TPU v7x, 256 devices: a whole 4x4x8 slice. The times are simulated.
256 devices in a mesh: wa: 64 (over x_hi, y, z), ba: 4 (over x_lo, core).
Axes of the slice: x: 4 (x_hi: 2, x_lo: 2; x = x_hi * 2 + x_lo), y: 4, z: 8, core: 2. Of those that a mesh axis runs over, the one named last changes fastest.
Arguments:
- latent: float32 [16, 8, 8192], P('ba', None, 'wa'), parts along dimension 0, may hold values from -12 to 12
- noise: float32 [2, 16, 8, 8192], P(None, 'ba', None, 'wa'), parts along dimension 1, may hold values from -6 to 6
- offsets: int32 [128], P('wa'), may hold values from 0 to 63
- anchors: int32 [2], replicated, may hold values from 0 to 127
- guidance: float32 [1], replicated, may hold values from 0.4 to 0.8
- w_in: bfloat16 [320, 36], replicated, may hold values from -1 to 1
- w_mid: bfloat16 [320, 320], replicated, may hold values from -0.3125 to 0.3125
- w_out: bfloat16 [36, 320], replicated, may hold values from -0.109375 to 0.109375
- t_embed: float32 [2, 320], replicated, may hold values from -6 to 6
- w_feat: float32 [64, 4], replicated, may hold values from -3 to 3
Outputs:
- denoised: float32 [16, 8, 8192], P('ba', None, 'wa'), parts along dimension 0
There are 4 independent parts, one for each index of `ba`. A program takes and returns all parts, laid end to end along the dimension named above; an argument that names none is the same for every part. Nothing has to cross between parts.
All inputs are finite; a program needn't handle non-finite values.
Results may differ from a plain program's by a relative error of at most 0.0065.
Values sent between devices are 32-bit elements; how exact they have to be, the bound alone decides.
A program may use at most 64 MiB of HBM per device.

v0:
```python
import math

import jax
import jax.numpy as jnp
from jax import lax
from jax.sharding import Mesh
from jax.sharding import PartitionSpec as P

WIN = 128
STRIDE = 64
STEPS = 2
WA = ("wa_0", "wa_1", "wa_2")


TAP_SHIFTS = ((-1, -1), (-1, 0), (-1, 1), (0, -1), (0, 0), (0, 1), (1, -1), (1, 0), (1, 1))
CUMULATIVE_ALPHA = (0.35, 0.55, 0.72, 0.85, 0.93)
STABILITY = 1e-06


def broadcast_by_axis(shard, axes, root):
    shard = jnp.where(lax.axis_index(axes) == root, shard, jnp.zeros_like(shard))
    for axis in axes:
        shard = lax.psum(shard, axis)
    return shard


def from_everyone(shard, axis):
    copies = jnp.broadcast_to(shard, (lax.axis_size(axis), *shard.shape))
    return lax.all_to_all(copies, axis, split_axis=0, concat_axis=0, tiled=True)


def of_everyone(shard, axis):
    return from_everyone(shard, axis).sum(axis=0)


def passed_along(shard, axis, by):
    length = lax.axis_size(axis)
    return lax.ppermute(shard, axis, [(i, (i + by) % length) for i in range(length)])


def plan(number):
    current = CUMULATIVE_ALPHA[number]
    following = CUMULATIVE_ALPHA[number + 1]
    spread = 0.3 * math.sqrt(1.0 - following)
    return (
        math.sqrt(current),
        math.sqrt(1.0 - current),
        math.sqrt(following),
        math.sqrt(1.0 - following - spread * spread),
        spread,
    )


def tapped(field):
    height, columns = (field.shape[-2], field.shape[-1])
    padding = [(0, 0)] * (field.ndim - 2) + [(1, 1), (1, 1)]
    padded = jnp.pad(field, padding)
    return jnp.stack(
        [
            padded[..., 1 + down_by : 1 + down_by + height, 1 + right_by : 1 + right_by + columns]
            for down_by, right_by in TAP_SHIFTS
        ]
    )


def denoise(window, w_in, w_mid, w_out, embedding):
    channels, height, columns = window.shape
    stacked = tapped(window.astype(jnp.bfloat16)).reshape(9 * channels, height * columns)
    hidden_in = jnp.dot(w_in, stacked, preferred_element_type=jnp.float32) + embedding[:, None]
    activated = jax.nn.silu(hidden_in).astype(jnp.bfloat16)
    middle = jnp.dot(w_mid, activated, preferred_element_type=jnp.float32)
    joined = (hidden_in + jax.nn.silu(middle)).astype(jnp.bfloat16)
    outward = jnp.dot(w_out, joined, preferred_element_type=jnp.float32).reshape(
        9, channels, height, columns
    )
    padded = jnp.pad(outward, ((0, 0), (0, 0), (1, 1), (1, 1)))
    result = jnp.zeros((channels, height, columns), jnp.float32)
    for index, (down_by, right_by) in enumerate(TAP_SHIFTS):
        result = (
            result
            + padded[
                index, :, 1 + down_by : 1 + down_by + height, 1 + right_by : 1 + right_by + columns
            ]
        )
    return result


def clean_of(windows, w_in, w_mid, w_out, embedding, now_a, now_s):
    predicted = jax.vmap(denoise, (0, None, None, None, None))(
        windows, w_in, w_mid, w_out, embedding
    )
    cleaned = (windows - now_s * predicted) / now_a
    return (cleaned, predicted)


def percept(cleaned, w_feat):
    return jax.nn.silu(jnp.einsum("fc,chw->fhw", w_feat, cleaned, precision=lax.Precision.HIGHEST))


def mismatch(cleaned, anchor_percept, w_feat):
    difference = percept(cleaned, w_feat) - anchor_percept
    return 0.5 * jnp.sum(difference * difference) / w_feat.shape[0]


def finish_gradient(cleaned, pullback, anchor_percept, w_feat):
    clean_grad = jax.vmap(jax.grad(mismatch), (0, None, None))(cleaned, anchor_percept, w_feat)
    return pullback(clean_grad)[0]


def advance(windows, gradient, predicted, scale, now_a, now_s, next_a, direction):
    return next_a * (windows - scale * gradient - now_s * predicted) / now_a + direction * predicted


def window_update(extended, number, starts, anchors, guidance, w_in, w_mid, w_out, t_embed, w_feat):
    per_dev = starts.shape[0]
    now_a, now_s, next_a, direction, spread = plan(number)
    embedding = t_embed[number]
    windows = jnp.stack(
        [lax.dynamic_slice_in_dim(extended, starts[index], WIN, 2) for index in range(per_dev)]
    )

    def cleaning(inputs):
        return clean_of(inputs, w_in, w_mid, w_out, embedding, now_a, now_s)

    cleaned, pullback, predicted = jax.vjp(cleaning, windows, has_aux=True)
    owner = anchors[number] // per_dev
    slot = anchors[number] % per_dev
    picked = lax.dynamic_index_in_dim(cleaned, slot, 0, keepdims=False)
    anchor_percept = percept(broadcast_by_axis(picked, WA, owner), w_feat)
    gradient = finish_gradient(cleaned, pullback, anchor_percept, w_feat)
    square_sum = of_everyone(jnp.sum(gradient * gradient), WA)
    element_count = per_dev * lax.axis_size(WA) * windows.shape[1] * windows.shape[2] * WIN
    scale = guidance[0] * lax.rsqrt(square_sum / element_count + STABILITY)
    advanced = advance(windows, gradient, predicted, scale, now_a, now_s, next_a, direction)
    summed = jnp.zeros(extended.shape, jnp.float32)
    for index in range(per_dev):
        current = lax.dynamic_slice_in_dim(summed, starts[index], WIN, 2)
        summed = lax.dynamic_update_slice_in_dim(
            summed, current + advanced[index], starts[index], 2
        )
    return (summed, spread)


def local(latent, noise, offsets, anchors, guidance, w_in, w_mid, w_out, t_embed, w_feat):
    width = latent.shape[-1]
    per_dev = offsets.shape[0]
    starts = jnp.arange(per_dev, dtype=jnp.int32) * STRIDE + offsets
    positions = jnp.arange(2 * width, dtype=jnp.int32)
    inside = (positions[None, :] >= starts[:, None]) & (positions[None, :] < starts[:, None] + WIN)
    cover = jnp.sum(inside.astype(jnp.float32), axis=0)
    count_own = cover[:width] + passed_along(cover[width:], WA, 1)
    state = latent
    for number in range(STEPS):
        neighbour = passed_along(state, WA, -1)
        extended = jnp.concatenate([state, neighbour], axis=2)
        summed, spread = window_update(
            extended, number, starts, anchors, guidance, w_in, w_mid, w_out, t_embed, w_feat
        )
        spill = passed_along(summed[:, :, width:], WA, 1)
        state = (summed[:, :, :width] + spill) / count_own + spread * noise[number]
    return state


def solution(mesh):
    finer = Mesh(mesh.devices.reshape(2, 4, 8, mesh.shape["ba"]), ("wa_0", "wa_1", "wa_2", "ba"))
    placed = (P("ba", None, WA), P(None, "ba", None, WA), P(WA), P(), P(), P(), P(), P(), P(), P())
    return jax.shard_map(
        local, mesh=finer, in_specs=placed, out_specs=P("ba", None, WA), check_vma=False
    )
```

profile of v0, /device:TPU:2, one launch (start us, length us, event | category | flops | bytes accessed | tf_op | source)
XLA Modules:
  0.0 238.8 jit_solution(6218011149825673397)
XLA Ops:
  0.8 9.9 %collective-permute-start = (f32[4,8,128]{2,0,1:T(4,128)S(1)}, f32[4,8,128]{2,0,1:T(4,128)S(1)}, u32[]{:S(2)}, u32[]{:S(2)}) collective-permute-start(f32[4,8,128]{2,0,1:T(4,128)S(1)} %get-tuple-element.43), channel_id=1, source_target_pairs={{0,252},{4,0},{8,4},{12,8},{16,12},{20,16},{24,20},{28,24},{32,28}... | collective-permute-start | bytes 49160 | tf_op jit(solution)/shard_map/ppermute | solution.py:38
  12.6 1.4 slice_reduce_fusion
  13.9 1.4 fusion.240
  22.8 1.3 fusion.190
  24.1 2.6 %fusion.88 = f32[2,1024,320]{1,2,0:T(8,128)} fusion(f32[2,1024,320]{1,2,0:T(8,128)S(1)} %fusion.190, f32[320]{0:T(512)S(1)} %get-tuple-element.6, bf16[320,320]{1,0:T(8,128)(2,1)S(1)} %copy-done), kind=kOutput, calls=%fused_computation.107 | convolution fusion | flops 423362560 | bytes 5448960 | tf_op jit(solution)/shard_map/jvp(vmap())/dot_general | solution.py:71
  26.7 2.6 %fusion.94 = f32[2,36,1024]{2,1,0:T(8,128)S(1)} fusion(f32[2,1024,320]{1,2,0:T(8,128)} %fusion.88, f32[2,1024,320]{1,2,0:T(8,128)S(1)} %fusion.190, f32[320]{0:T(512)S(1)} %get-tuple-element.6, bf16[36,320]{1,0:T(8,128)(2,1)S(1)} %copy-done.3), kind=kOutput, calls=%fused_computation.112 | convolution fusion | flops 51773440 | bytes 5562112 | tf_op jit(solution)/shard_map/jvp(vmap())/dot_general | solution.py:73
  29.7 9.6 %psum.42 = f32[4,8,128]{2,0,1:T(4,128)S(1)} all-reduce(f32[4,8,128]{2,0,1:T(4,128)S(1)} %select_bitcast_fusion.1), channel_id=1, replica_groups=mesh['wa_0'=2,'wa_1'=4,'wa_2'=8,'ba'=4] {'wa_0'}, use_global_device_ids=true, to_apply=%region_0.0 | all-reduce | flops 4096 | bytes 32768 | tf_op jit(solution)/shard_map/psum | solution.py:23
  39.2 14.3 %psum.43 = f32[4,8,128]{2,0,1:T(4,128)S(1)} all-reduce(f32[4,8,128]{2,0,1:T(4,128)S(1)} %psum.42), channel_id=1, replica_groups=mesh['wa_0'=2,'wa_1'=4,'wa_2'=8,'ba'=4] {'wa_1'}, use_global_device_ids=true, to_apply=%region_1.2 | all-reduce | flops 4096 | bytes 32768 | tf_op jit(solution)/shard_map/psum | solution.py:23
  53.5 34.2 %psum.44 = f32[4,8,128]{2,0,1:T(4,128)S(1)} all-reduce(f32[4,8,128]{2,0,1:T(4,128)S(1)} %psum.43), channel_id=1, replica_groups=mesh['wa_0'=2,'wa_1'=4,'wa_2'=8,'ba'=4] {'wa_2'}, use_global_device_ids=true, to_apply=%region_2.3 | all-reduce | flops 4096 | bytes 32768 | tf_op jit(solution)/shard_map/psum | solution.py:23
  87.7 1.3 convolution_bitcast_fusion.1
  89.0 1.1 divide_multiply_fusion.1
  91.4 1.6 convolution_convert_fusion.1
  93.0 5.1 %fusion.110 = bf16[2,36,1024]{2,1,0:T(8,128)(2,1)S(1)} fusion(bf16[2,1024,320]{1,2,0:T(8,128)(2,1)} %convolution_convert_fusion.1, f32[2,1024,320]{1,2,0:T(8,128)S(1)} %fusion.190, f32[2,1024,320]{1,2,0:T(8,128)} %fusion.88, f32[320]{0:T(512)S(1)} %copy-done.13, bf16[320,320]{1,0:T(8,128)(2,1)S(1)} %copy-done, bf16[320,36]{0,1:T(8,128)(2,1)S(1)} %copy-done.1), kind=kOutput, calls=%fused_computation.118 | convolution fusion | flops 482418688 | bytes 6930176 | tf_op jit(solution)/shard_map/transpose(jvp(vmap()))/dot_general | solution.py:69
  99.2 1.3 broadcast_in_dim.9
  100.4 4.8 %all-to-all-start = ((f32[64,1,1]{2,1,0:T(1,128)}), f32[64,1,1]{2,1,0:T(1,128)S(1)}, u32[]{:S(2)}, u32[]{:S(2)}) async-start(f32[64,1,1]{2,1,0:T(1,128)} %broadcast_in_dim.9), calls=%async_computation | async-start | bytes 65536 | tf_op jit(solution)/shard_map/all_to_all | solution.py:29
  106.5 10.6 %all-to-all-done = f32[64,1,1]{2,1,0:T(1,128)S(1)} async-done(((f32[64,1,1]{2,1,0:T(1,128)}), f32[64,1,1]{2,1,0:T(1,128)S(1)}, u32[]{:S(2)}, u32[]{:S(2)}) %all-to-all-start) | async-done | bytes 288 | tf_op jit(solution)/shard_map/all_to_all | solution.py:29
  118.5 1.3 dynamic_update_slice.12
  119.9 1.3 dynamic_update_slice.13
  122.5 8.3 %collective-permute-done.1 = f32[4,8,128]{2,0,1:T(4,128)S(1)} collective-permute-done((f32[4,8,128]{2,0,1:T(4,128)S(1)}, f32[4,8,128]{2,0,1:T(4,128)S(1)}, u32[]{:S(2)}, u32[]{:S(2)}) %collective-permute-start.1) | collective-permute-done | bytes 16416 | tf_op jit(solution)/shard_map/ppermute | solution.py:38
  133.4 1.2 collective-permute-done.3
  137.2 1.5 copy-done.16
  140.0 1.3 convolution_bitcast_fusion
  141.3 8.9 %psum.45 = f32[4,8,128]{2,0,1:T(4,128)S(1)} all-reduce(f32[4,8,128]{2,0,1:T(4,128)S(1)} %select_bitcast_fusion), channel_id=1, replica_groups=mesh['wa_0'=2,'wa_1'=4,'wa_2'=8,'ba'=4] {'wa_0'}, use_global_device_ids=true, to_apply=%region_6.7 | all-reduce | flops 4096 | bytes 32768 | tf_op jit(solution)/shard_map/psum | solution.py:23
  150.2 14.3 %psum.46 = f32[4,8,128]{2,0,1:T(4,128)S(1)} all-reduce(f32[4,8,128]{2,0,1:T(4,128)S(1)} %psum.45), channel_id=1, replica_groups=mesh['wa_0'=2,'wa_1'=4,'wa_2'=8,'ba'=4] {'wa_1'}, use_global_device_ids=true, to_apply=%region_7.8 | all-reduce | flops 4096 | bytes 32768 | tf_op jit(solution)/shard_map/psum | solution.py:23
  164.5 32.8 %psum.47 = f32[4,8,128]{2,0,1:T(4,128)S(1)} all-reduce(f32[4,8,128]{2,0,1:T(4,128)S(1)} %psum.46), channel_id=1, replica_groups=mesh['wa_0'=2,'wa_1'=4,'wa_2'=8,'ba'=4] {'wa_2'}, use_global_device_ids=true, to_apply=%region_8.9 | all-reduce | flops 4096 | bytes 32768 | tf_op jit(solution)/shard_map/psum | solution.py:23
  198.5 1.3 fusion.120
  200.4 1.6 convolution_convert_fusion
  202.1 5.1 %fusion.115 = bf16[2,36,1024]{2,1,0:T(8,128)(2,1)S(1)} fusion(bf16[2,1024,320]{1,2,0:T(8,128)(2,1)} %convolution_convert_fusion, f32[2,1024,320]{1,2,0:T(8,128)S(1)} %fusion.187, f32[2,1024,320]{1,2,0:T(8,128)} %copy-done.16, f32[320]{0:T(512)S(1)} %copy-done.11, bf16[320,320]{1,0:T(8,128)(2,1)S(1)} %copy-done, bf16[320,36]{0,1:T(8,128)(2,1)S(1)} %copy-done.2), kind=kOutput, calls=%fused_computation.119 | convolution fusion | flops 482418688 | bytes 6930176 | tf_op jit(solution)/shard_map/transpose(jvp(vmap()))/dot_general | solution.py:69
  208.8 15.8 %all_to_all.12 = f32[64,1,1]{2,1,0:T(1,128)S(1)} all-to-all(f32[64,1,1]{2,1,0:T(1,128)S(1)} %broadcast_in_dim.11), channel_id=1, replica_groups=mesh['wa_0'=2,'wa_1'=4,'wa_2'=8,'ba'=4] {'wa_0','wa_1','wa_2'}, dimensions={0} | all-to-all | bytes 512 | tf_op jit(solution)/shard_map/all_to_all | solution.py:29
  225.9 1.3 dynamic_update_slice.14
  227.3 1.3 dynamic_update_slice.15
  229.4 8.8 %collective-permute-done.4 = f32[4,8,128]{2,0,1:T(4,128)S(1)} collective-permute-done((f32[4,8,128]{2,0,1:T(4,128)S(1)}, f32[4,8,128]{2,0,1:T(4,128)S(1)}, u32[]{:S(2)}, u32[]{:S(2)}) %collective-permute-start.4) | collective-permute-done | bytes 16416 | tf_op jit(solution)/shard_map/ppermute | solution.py:38
  (124 shorter events, 18.1 us)
Async XLA Ops:
  0.0 24.1 %copy-start = (bf16[320,320]{1,0:T(8,128)(2,1)S(1)}, bf16[320,320]{1,0:T(8,128)(2,1)}, u32[]{:S(2)}) copy-start(bf16[320,320]{1,0:T(8,128)(2,1)} %param.16) | copy-start | bytes 614404
  0.8 21.1 %collective-permute-start = (f32[4,8,128]{2,0,1:T(4,128)S(1)}, f32[4,8,128]{2,0,1:T(4,128)S(1)}, u32[]{:S(2)}, u32[]{:S(2)}) collective-permute-start(f32[4,8,128]{2,0,1:T(4,128)S(1)} %get-tuple-element.43), channel_id=1, source_target_pairs={{0,252},{4,0},{8,4},{12,8},{16,12},{20,16},{24,20},{28,24},{32,28}... | collective-permute-start | bytes 49160 | tf_op jit(solution)/shard_map/ppermute | solution.py:38
  11.4 1.2 copy-start.14
  12.0 110.0 %collective-permute-start.2 = (f32[128]{0:T(128)}, f32[128]{0:T(128)}, u32[]{:S(2)}, u32[]{:S(2)}) collective-permute-start(f32[128]{0:T(128)} %slice.200), channel_id=1, source_target_pairs={{0,4},{4,8},{8,12},{12,16},{16,20},{20,24},{24,28},{28,32},{32,36}... | collective-permute-start | bytes 1544 | tf_op jit(solution)/shard_map/ppermute | solution.py:38
  13.9 12.7 %copy-start.12 = (f32[320]{0:T(512)}, f32[320]{0:T(512)S(1)}, u32[]{:S(2)}) copy-start(f32[320]{0:T(512)S(1)} %get-tuple-element.6) | copy-start | bytes 3844
  24.1 2.6 %copy-start.3 = (bf16[36,320]{1,0:T(8,128)(2,1)S(1)}, bf16[36,320]{1,0:T(8,128)(2,1)}, u32[]{:S(2)}) copy-start(bf16[36,320]{1,0:T(8,128)(2,1)} %param.17) | copy-start | bytes 69124
  29.4 60.8 %copy-start.7 = (f32[64,4]{0,1:T(4,128)S(1)}, f32[64,4]{0,1:T(4,128)}, u32[]{:S(2)}) copy-start(f32[64,4]{0,1:T(4,128)} %param.19) | copy-start | bytes 3076
  90.2 2.9 %copy-start.1 = (bf16[320,36]{0,1:T(8,128)(2,1)S(1)}, bf16[320,36]{0,1:T(8,128)(2,1)}, u32[]{:S(2)}) copy-start(bf16[320,36]{0,1:T(8,128)(2,1)} %param.15) | copy-start | bytes 69124
  90.2 2.8 %copy-start.13 = (f32[320]{0:T(512)S(1)}, f32[320]{0:T(512)}, u32[]{:S(2)}) copy-start(f32[320]{0:T(512)} %copy-done.12) | copy-start | bytes 3844
  93.0 12.2 %copy-start.6 = (f32[2,4,8,128]{3,2,1,0:T(8,128)S(1)}, f32[2,4,8,128]{3,2,1,0:T(8,128)}, u32[]{:S(2)}) copy-start(f32[2,4,8,128]{3,2,1,0:T(8,128)} %param.11) | copy-start | bytes 98308
  93.0 28.9 %copy-start.15 = (f32[256]{0:T(256)S(1)}, f32[256]{0:T(256)}, u32[]{:S(2)}) copy-start(f32[256]{0:T(256)} %copy-done.14) | copy-start | bytes 3076
  98.3 37.9 %copy-start.10 = (f32[320]{0:T(512)S(1)}, f32[320]{0:T(512)}, u32[]{:S(2)}) copy-start(f32[320]{0:T(512)} %get-tuple-element.5) | copy-start | bytes 3844
  100.4 16.6 %all-to-all-start = ((f32[64,1,1]{2,1,0:T(1,128)}), f32[64,1,1]{2,1,0:T(1,128)S(1)}, u32[]{:S(2)}, u32[]{:S(2)}) async-start(f32[64,1,1]{2,1,0:T(1,128)} %broadcast_in_dim.9), calls=%async_computation | async-start | bytes 65536 | tf_op jit(solution)/shard_map/all_to_all | solution.py:29
  121.2 9.5 %collective-permute-start.1 = (f32[4,8,128]{2,0,1:T(4,128)S(1)}, f32[4,8,128]{2,0,1:T(4,128)S(1)}, u32[]{:S(2)}, u32[]{:S(2)}) collective-permute-start(f32[4,8,128]{2,0,1:T(4,128)S(1)} %slice.230), channel_id=1, source_target_pairs={{0,4},{4,8},{8,12},{12,16},{16,20},{20,24},{24,28},{28,32},{32,36}... | collective-permute-start | bytes 49160 | tf_op jit(solution)/shard_map/ppermute | solution.py:38
  122.5 10.9 %copy-start.8 = (f32[128]{0:T(128)}, f32[128]{0:T(128)S(1)}, u32[]{:S(2)}) copy-start(f32[128]{0:T(128)S(1)} %slice_add_fusion.2) | copy-start | bytes 1540
  130.8 3.8 %collective-permute-start.3 = (f32[4,8,128]{2,0,1:T(4,128)S(1)}, f32[4,8,128]{2,0,1:T(4,128)S(1)}, u32[]{:S(2)}, u32[]{:S(2)}) collective-permute-start(f32[4,8,128]{2,0,1:T(4,128)S(1)} %divide_add_fusion.1), channel_id=1, source_target_pairs={{0,252},{4,0},{8,4},{12,8},{16,12},{20,16},{24,20},{28,24},{32,28}... | collective-permute-start | bytes 49160 | tf_op jit(solution)/shard_map/ppermute | solution.py:38
  137.2 1.5 copy-start.16
  198.5 1.9 copy-start.4
  198.5 3.6 %copy-start.2 = (bf16[320,36]{0,1:T(8,128)(2,1)S(1)}, bf16[320,36]{0,1:T(8,128)(2,1)}, u32[]{:S(2)}) copy-start(bf16[320,36]{0,1:T(8,128)(2,1)} %param.15) | copy-start | bytes 69124
  199.8 2.2 copy-start.11
  202.0 36.1 %copy-start.5 = (f32[1,4,8,128]{3,2,1,0:T(8,128)S(1)}, f32[1,4,8,128]{3,2,1,0:T(8,128)}, u32[]{:S(2)}) copy-start(f32[1,4,8,128]{3,2,1,0:T(8,128)} %get-tuple-element.42) | copy-start | bytes 49156
  202.0 36.1 %copy-start.9 = (f32[128]{0:T(128)S(1)}, f32[128]{0:T(128)}, u32[]{:S(2)}) copy-start(f32[128]{0:T(128)} %copy-done.8) | copy-start | bytes 1540
  228.6 9.5 %collective-permute-start.4 = (f32[4,8,128]{2,0,1:T(4,128)S(1)}, f32[4,8,128]{2,0,1:T(4,128)S(1)}, u32[]{:S(2)}, u32[]{:S(2)}) collective-permute-start(f32[4,8,128]{2,0,1:T(4,128)S(1)} %slice.235), channel_id=1, source_target_pairs={{0,4},{4,8},{8,12},{12,16},{16,20},{20,24},{24,28},{28,32},{32,36}... | collective-permute-start | bytes 49160 | tf_op jit(solution)/shard_map/ppermute | solution.py:38
where the time goes:
time: 240 us; the launch traced here: 239 us
  blocking collectives  130 us (54%)
  matrix products  29.2 us (12%)
  waiting for transfers between devices  28.9 us (12%)
  local copies, waits for them, and re-layouts  16.4 us (7%)
  starting transfers between devices  16.1 us (7%)
  between operations  11.6 us (5%)
  other arithmetic  6.67 us (3%)
    psum x6, blocking collectives, broadcast_by_axis(): shard = lax.psum(shard, axis)  114 us
    ppermute x5, waiting for transfers between devices, passed_along(): lax.ppermute(shard, axis, [(i, (i + by) % length) for i in range(length)])  18.3 us
    all_to_all x1, blocking collectives, from_everyone(): return lax.all_to_all(copies, axis, split_axis=0, concat_axis=0, tiled=True)  15.8 us
    dot_general x4, matrix products, denoise(): jnp.dot(w_in, stacked, preferred_element_type=jnp.float32)  12 us
    ppermute x5, starting transfers between devices, passed_along(): lax.ppermute(shard, axis, [(i, (i + by) % length) for i in range(length)])  11.3 us
    all_to_all x1, waiting for transfers between devices, from_everyone(): return lax.all_to_all(copies, axis, split_axis=0, concat_axis=0, tiled=True)  10.6 us
    dot_general x6, matrix products, percept(): jnp.einsum('fc,chw->fhw', w_feat, cleaned, precision=lax.Precision.HIGHEST)  6.83 us
    dot_general x4, matrix products, denoise(): jnp.dot(w_out, joined, preferred_element_type=jnp.float32)  6.8 us
  transfers between devices with their start and end apart: 6, of which 4 were waited for; matrix products, arithmetic and copies ran while one was open for 12% of the time, Pallas kernels for 0%

commit v1 on v0

v1 whole, which is shorter than its diff:
```python
import functools
import math

import jax
import jax.numpy as jnp
from jax import lax
from jax.experimental import pallas as pl
from jax.experimental.pallas import tpu as pltpu
from jax.sharding import PartitionSpec as P

WIN = 128
STRIDE = 64
STEPS = 2
ROWS = 8
HEIGHT = 8
HALF = 4
HID = 320
FEAT = 64
TAPROWS = 80
CHUNK = 256
MESH = pl.DeviceIdType.MESH
F32 = jnp.float32
BF16 = jnp.bfloat16

TAP_SHIFTS = ((-1, -1), (-1, 0), (-1, 1), (0, -1), (0, 0), (0, 1), (1, -1), (1, 0), (1, 1))
CUMULATIVE_ALPHA = (0.35, 0.55, 0.72, 0.85, 0.93)
STABILITY = 1e-06


def plan(number):
    current = CUMULATIVE_ALPHA[number]
    following = CUMULATIVE_ALPHA[number + 1]
    spread = 0.3 * math.sqrt(1.0 - following)
    return (
        math.sqrt(current),
        math.sqrt(1.0 - current),
        math.sqrt(following),
        math.sqrt(1.0 - following - spread * spread),
        spread,
    )


def group_sizes(count):
    inner = 8 if count % 8 == 0 else 2
    return inner, count // inner


def lane_iota():
    return lax.broadcasted_iota(jnp.int32, (ROWS, WIN), 1)


def row_iota():
    return lax.broadcasted_iota(jnp.int32, (ROWS, WIN), 0)


def sideways(tile, by):
    if by == 0:
        return tile
    lanes = lane_iota()
    if by == 1:
        return jnp.where(lanes < WIN - 1, pltpu.roll(tile, WIN - 1, 1), 0.0)
    return jnp.where(lanes > 0, pltpu.roll(tile, 1, 1), 0.0)


def swapped(tile):
    return pltpu.roll(tile, 4, 0)


def low_high(low, high):
    return jnp.where(row_iota() < 4, low, high)


def store_taps(ref, tiles, sign):
    by_shift = {by: [sideways(tile, by) for tile in tiles] for by in (-1, 0, 1)}
    zero = jnp.zeros((ROWS, WIN), F32)

    def piece(k, h):
        if k >= len(TAP_SHIFTS):
            return zero
        down_by, right_by = TAP_SHIFTS[k]
        at = h + sign * down_by
        if at < 0 or at >= HEIGHT:
            return zero
        return by_shift[sign * right_by][at]

    for h in range(HEIGHT):
        for pair in range(TAPROWS // 16):
            both = jnp.concatenate([piece(2 * pair, h), piece(2 * pair + 1, h)], axis=0)
            ref[16 * pair : 16 * pair + 16, h * WIN : (h + 1) * WIN] = both.astype(BF16)


def summed_taps(ref, sign, rounded):
    tiles = []
    for h in range(HEIGHT):
        by_shift = {}
        for k, (down_by, right_by) in enumerate(TAP_SHIFTS):
            at = h + sign * down_by
            if at < 0 or at >= HEIGHT:
                continue
            value = ref[8 * k : 8 * k + 8, at * WIN : (at + 1) * WIN]
            if rounded:
                value = value.astype(BF16).astype(F32)
            shift = sign * right_by
            by_shift[shift] = value if shift not in by_shift else by_shift[shift] + value
        tiles.append(
            by_shift[0] + sideways(by_shift[-1], -1) + sideways(by_shift[1], 1)
        )
    return tiles


def gate_of(value):
    return 0.5 * jnp.tanh(0.5 * value) + 0.5


def dot(left, right):
    return jnp.dot(left, right, preferred_element_type=F32)


def dot_nt(left, right):
    return lax.dot_general(
        left, right, (((1,), (1,)), ((), ())), preferred_element_type=F32
    )


def kernel(
    count,
    latent_ref,
    noise_ref,
    offsets_ref,
    anchors_ref,
    guidance_ref,
    w_in_ref,
    w_mid_ref,
    w_out_ref,
    t_embed_ref,
    w_feat_ref,
    out_ref,
    win_ref,
    wint_ref,
    wout_ref,
    woutt_ref,
    wmidt_ref,
    embed_ref,
    feat_ref,
    taps_ref,
    outward_ref,
    d1_ref,
    d2_ref,
    hid_ref,
    percept_ref,
    halo_src,
    halo_dst,
    cover_src,
    cover_dst,
    sums_left_src,
    sums_left_dst,
    sums_right_src,
    sums_right_dst,
    cast_src,
    cast_mid,
    cast_first,
    cast_second,
    square_src,
    square_mid,
    square_first,
    square_second,
    edge_send,
    edge_recv,
    cast_send,
    cast_recv,
    square_send,
    square_recv,
):
    inner, outer = group_sizes(count)
    me = lax.axis_index("wa")
    part = lax.axis_index("ba")
    my_inner = lax.rem(me, inner)
    my_outer = me // inner
    right = lax.rem(me + 1, count)
    left = lax.rem(me + count - 1, count)

    def inner_peer(by):
        return my_outer * inner + lax.rem(my_inner + by, inner)

    def outer_peer(by):
        return lax.rem(my_outer + by, outer) * inner + my_inner

    barrier = pltpu.get_barrier_semaphore()
    peers = [inner_peer(by) for by in range(1, inner)]
    peers += [outer_peer(by) for by in range(1, outer)]
    peers += [left, right]
    for peer in peers:
        pl.semaphore_signal(barrier, inc=1, device_id=(peer, part), device_id_type=MESH)

    def remote(source, target, send, recv, peer):
        return pltpu.make_async_remote_copy(
            src_ref=source,
            dst_ref=target,
            send_sem=send,
            recv_sem=recv,
            device_id=(peer, part),
            device_id_type=MESH,
        )

    lanes = lane_iota()
    starts = [slot * STRIDE + offsets_ref[slot] for slot in range(2)]

    def packed(ref, base):
        return [
            jnp.concatenate(
                [
                    ref[pl.ds(base + tile, 4, stride=8), :],
                    ref[pl.ds(base + tile + HALF, 4, stride=8), :],
                ],
                axis=0,
            )
            for tile in range(HALF)
        ]

    own = packed(latent_ref, 0)
    noise = [packed(noise_ref, 32 * number) for number in range(STEPS)]
    for tile in range(HALF):
        halo_src[0, :, tile * WIN : (tile + 1) * WIN] = own[tile]
        halo_src[1, :, tile * WIN : (tile + 1) * WIN] = noise[0][tile]
    cover_own = sum(jnp.where(lanes >= start, 1.0, 0.0) for start in starts)
    cover_next = sum(jnp.where(lanes < start, 1.0, 0.0) for start in starts)
    cover_src[0] = cover_own
    cover_src[1] = cover_next

    pl.semaphore_wait(barrier, len(peers))

    copies = [
        remote(halo_src.at[0], halo_dst.at[0], edge_send.at[0], edge_recv.at[0], left),
        remote(halo_src.at[1], halo_dst.at[1], edge_send.at[1], edge_recv.at[1], left),
        remote(cover_src.at[0], cover_dst.at[0], edge_send.at[2], edge_recv.at[2], left),
        remote(cover_src.at[1], cover_dst.at[1], edge_send.at[3], edge_recv.at[3], right),
    ]
    for copy in copies:
        copy.start()

    def one_hot(shape, rows_first, slot):
        wide = lax.broadcasted_iota(jnp.int32, shape, 0 if rows_first else 1)
        small = lax.broadcasted_iota(jnp.int32, shape, 1 if rows_first else 0)
        tap = small // 4
        return jnp.where(wide == tap * 8 + slot * 4 + (small - tap * 4), 1.0, 0.0).astype(BF16)

    eye = jnp.where(
        lax.broadcasted_iota(jnp.int32, (HID, HID), 0)
        == lax.broadcasted_iota(jnp.int32, (HID, HID), 1),
        1.0,
        0.0,
    )
    eye_b = eye.astype(BF16)
    w_in = w_in_ref[...]
    w_out = w_out_ref[...]
    for slot in range(2):
        spread_rows = one_hot((TAPROWS, 36), True, slot)
        spread_columns = one_hot((36, TAPROWS), False, slot)
        win_ref[slot] = dot(w_in, spread_columns).astype(BF16)
        wint_ref[slot] = dot_nt(spread_rows, w_in).astype(BF16)
        wout = dot(spread_rows, w_out).astype(BF16)
        wout_ref[slot] = wout
        woutt_ref[slot] = dot_nt(eye_b, wout).astype(BF16)
    wmidt_ref[...] = dot_nt(eye_b, w_mid_ref[...]).astype(BF16)
    for number in range(STEPS):
        column = jnp.sum(eye * t_embed_ref[number : number + 1, :], axis=1, keepdims=True)
        embed_ref[number] = jnp.broadcast_to(column, (HID, WIN))
    for channel in range(4):
        feat_ref[channel] = jnp.broadcast_to(w_feat_ref[:, channel : channel + 1], (FEAT, WIN))

    def denoised(tiles, number, slots, keep):
        store_taps(taps_ref, tiles, 1)

        def chunk(step, carry):
            at = pl.ds(pl.multiple_of(step * CHUNK, CHUNK), CHUNK)
            embedding = jnp.concatenate([embed_ref[number]] * (CHUNK // WIN), axis=1)
            taps = taps_ref[:, at]
            total = None
            for slot in slots:
                hidden = dot(win_ref[slot], taps) + embedding
                gate = gate_of(hidden)
                active = hidden * gate
                hid_ref[slot] = hidden
                if keep:
                    d1_ref[slot, :, at] = (gate + active * (1.0 - gate)).astype(BF16)
                middle = dot(w_mid_ref[...], active.astype(BF16))
                gate = gate_of(middle)
                active = middle * gate
                if keep:
                    d2_ref[slot, :, at] = (gate + active * (1.0 - gate)).astype(BF16)
                joined = (hid_ref[slot] + active).astype(BF16)
                outward = dot(wout_ref[slot], joined)
                total = outward if total is None else total + outward
            outward_ref[:, at] = total
            return carry

        lax.fori_loop(0, HEIGHT * WIN // CHUNK, chunk, 0)
        return summed_taps(outward_ref, 1, False)

    def pulled_back(tiles):
        store_taps(taps_ref, tiles, -1)

        def chunk(step, carry):
            at = pl.ds(pl.multiple_of(step * CHUNK, CHUNK), CHUNK)
            taps = taps_ref[:, at]
            total = None
            for slot in range(2):
                joined = dot(woutt_ref[slot], taps).astype(BF16).astype(F32)
                middle = (joined * d2_ref[slot, :, at].astype(F32)).astype(BF16)
                active = dot(wmidt_ref[...], middle).astype(BF16).astype(F32)
                hidden = (joined + active * d1_ref[slot, :, at].astype(F32)).astype(BF16)
                inward = dot(wint_ref[slot], hidden)
                total = inward if total is None else total + inward
            outward_ref[:, at] = total
            return carry

        lax.fori_loop(0, HEIGHT * WIN // CHUNK, chunk, 0)
        return summed_taps(outward_ref, -1, True)

    def features(tile, slot):
        total = None
        for channel in range(4):
            row = tile[slot * 4 + channel : slot * 4 + channel + 1, :]
            term = feat_ref[channel] * row
            total = term if total is None else total + term
        return total

    def windows_of(first, second):
        both = []
        for start in starts:
            back = lax.rem(WIN - start, WIN)
            both.append(
                [
                    jnp.where(
                        lanes < WIN - start,
                        pltpu.roll(first[tile], back, 1),
                        pltpu.roll(second[tile], back, 1),
                    )
                    for tile in range(HALF)
                ]
            )
        tiles = [low_high(both[0][tile], swapped(both[1][tile])) for tile in range(HALF)]
        tiles += [low_high(swapped(both[0][tile]), both[1][tile]) for tile in range(HALF)]
        return both, tiles

    def placed(tiles):
        own_sum, next_sum = [], []
        for tile in range(HALF):
            low, high = tiles[tile], tiles[tile + HALF]
            pieces = (low_high(low, swapped(high)), low_high(swapped(low), high))
            turned = [pltpu.roll(piece, start, 1) for piece, start in zip(pieces, starts)]
            own_sum.append(
                sum(jnp.where(lanes >= start, t, 0.0) for t, start in zip(turned, starts))
            )
            next_sum.append(
                sum(jnp.where(lanes < start, t, 0.0) for t, start in zip(turned, starts))
            )
        return own_sum, next_sum

    def all_of(ref, *index):
        return [ref[(*index, slice(None), slice(t * WIN, (t + 1) * WIN))] for t in range(HALF)]

    def far_first(size):
        return sorted(range(1, size), key=lambda by: -min(by, size - by))

    def exchange(number, phase, source, first, send_sem, recv_sem, halves):
        started = []
        for half in halves:
            along_inner = (half == 0) == (phase == 0)
            size = inner if along_inner else outer
            for by in far_first(size):
                peer = inner_peer(by) if along_inner else outer_peer(by)
                copy = remote(
                    source.at[number, half],
                    first.at[number, half, by - 1],
                    send_sem.at[number, phase, half, by - 1],
                    recv_sem.at[number, phase, half, by - 1],
                    peer,
                )
                copy.start()
                started.append((half, by, copy))
        return started

    def finish(number, started, source, first, halves):
        totals = {half: source[number, half] for half in halves}
        for half, by, copy in started:
            copy.wait_recv()
            totals[half] = totals[half] + first[number, half, by - 1]
        return totals

    copies[0].wait_recv()
    following = all_of(halo_dst, 0)
    sent = list(copies)
    for number in range(STEPS):
        now_a, now_s, next_a, direction, spread = plan(number)
        both, tiles = windows_of(own, following)

        anchor = anchors_ref[number]
        picks = [jnp.where(anchor == 2 * me + slot, 1.0, 0.0) for slot in range(2)]
        for tile in range(HALF):
            value = both[0][tile] * picks[0] + both[1][tile] * picks[1]
            cast_src[number, tile // 2, :, (tile % 2) * WIN : (tile % 2 + 1) * WIN] = value
        first = exchange(number, 0, cast_src, cast_first, cast_send, cast_recv, (0, 1))

        predicted = denoised(tiles, number, (0, 1), True)
        cleaned = [(x - now_s * p) * (1.0 / now_a) for x, p in zip(tiles, predicted)]
        base = [
            (next_a / now_a) * (x - now_s * p) + direction * p for x, p in zip(tiles, predicted)
        ]
        base_own, base_next = placed(base)

        totals = finish(number, first, cast_src, cast_first, (0, 1))
        for half in range(2):
            cast_mid[number, half] = totals[half]
        second = exchange(number, 1, cast_mid, cast_second, cast_send, cast_recv, (0, 1))
        totals = finish(number, second, cast_mid, cast_second, (0, 1))
        sent += [copy for _, _, copy in first + second]
        picked = [
            totals[tile // 2][:, (tile % 2) * WIN : (tile % 2 + 1) * WIN] for tile in range(HALF)
        ]
        anchor_tiles = picked + [swapped(tile) for tile in picked]
        anchor_predicted = denoised(anchor_tiles, number, (0,), False)
        for h in range(HEIGHT):
            clean = (anchor_tiles[h] - now_s * anchor_predicted[h]) * (1.0 / now_a)
            value = features(clean, 0)
            percept_ref[h] = value * gate_of(value)

        clean_grad = []
        for h in range(HEIGHT):
            grad = jnp.zeros((ROWS, WIN), F32)
            for slot in range(2):
                value = features(cleaned[h], slot)
                gate = gate_of(value)
                active = value * gate
                slope = gate + active * (1.0 - gate)
                pull = (active - percept_ref[h]) * slope * (1.0 / FEAT)
                for channel in range(4):
                    row = jnp.sum(feat_ref[channel] * pull, axis=0, keepdims=True)
                    grad = jnp.where(row_iota() == slot * 4 + channel, row, grad)
            clean_grad.append(grad)
        pulled = pulled_back([(-now_s / now_a) * grad for grad in clean_grad])
        gradient = [p + g * (1.0 / now_a) for p, g in zip(pulled, clean_grad)]

        squares = sum(g * g for g in gradient)
        square = jnp.sum(jnp.sum(squares, axis=1, keepdims=True), axis=0, keepdims=True)
        square_src[number, 0] = jnp.broadcast_to(square, (1, WIN))
        first = exchange(
            number, 0, square_src, square_first, square_send, square_recv, (0,)
        )

        grad_own, grad_next = placed(gradient)
        last = number == STEPS - 1
        for tile in range(HALF):
            at = slice(tile * WIN, (tile + 1) * WIN)
            if not last:
                sums_left_src[0, :, at] = base_own[tile]
                sums_left_src[1, :, at] = grad_own[tile]
            sums_right_src[number, 0, :, at] = base_next[tile]
            sums_right_src[number, 1, :, at] = grad_next[tile]
        to_right = remote(
            sums_right_src.at[number],
            sums_right_dst.at[number],
            edge_send.at[4 + number],
            edge_recv.at[4 + number],
            right,
        )
        to_right.start()
        sent.append(to_right)
        if not last:
            to_left = remote(
                sums_left_src, sums_left_dst, edge_send.at[6], edge_recv.at[6], left
            )
            to_left.start()
            sent.append(to_left)

        totals = finish(number, first, square_src, square_first, (0,))
        square_mid[number, 0] = totals[0]
        second = exchange(
            number, 1, square_mid, square_second, square_send, square_recv, (0,)
        )
        totals = finish(number, second, square_mid, square_second, (0,))
        sent += [copy for _, _, copy in first + second]
        entries = 2 * count * 4 * HEIGHT * WIN
        scale = guidance_ref[0] * lax.rsqrt(totals[0] * (1.0 / entries) + STABILITY)
        scale = (next_a / now_a) * scale

        if number == 0:
            for copy in copies[1:]:
                copy.wait_recv()
            per_own = 1.0 / (cover_own + cover_dst[1])
            per_next = 1.0 / (cover_next + cover_dst[0])
            noise_next = all_of(halo_dst, 1)
        to_right.wait_recv()
        base_in = all_of(sums_right_dst, number, 0)
        grad_in = all_of(sums_right_dst, number, 1)
        own = [
            (base_own[t] + base_in[t] - scale * (grad_own[t] + grad_in[t])) * per_own
            + spread * noise[number][t]
            for t in range(HALF)
        ]
        if not last:
            to_left.wait_recv()
            base_in = all_of(sums_left_dst, 0)
            grad_in = all_of(sums_left_dst, 1)
            following = [
                (base_next[t] + base_in[t] - scale * (grad_next[t] + grad_in[t])) * per_next
                + spread * noise_next[t]
                for t in range(HALF)
            ]

    for tile in range(HALF):
        out_ref[:, tile * WIN : (tile + 1) * WIN] = own[tile]
    for copy in sent:
        copy.wait_send()


def local(count, latent, noise, offsets, anchors, guidance, w_in, w_mid, w_out, t_embed, w_feat):
    inner, outer = group_sizes(count)
    most = max(inner, outer)
    vmem = pl.BlockSpec(memory_space=pltpu.VMEM)
    smem = pl.BlockSpec(memory_space=pltpu.SMEM)
    block = HALF * WIN
    dma = pltpu.SemaphoreType.DMA
    out = pl.pallas_call(
        functools.partial(kernel, count),
        out_shape=jax.ShapeDtypeStruct((ROWS, block), F32),
        in_specs=[vmem, vmem, smem, smem, smem, vmem, vmem, vmem, vmem, vmem],
        out_specs=vmem,
        scratch_shapes=[
            pltpu.VMEM((2, HID, TAPROWS), BF16),
            pltpu.VMEM((2, TAPROWS, HID), BF16),
            pltpu.VMEM((2, TAPROWS, HID), BF16),
            pltpu.VMEM((2, HID, TAPROWS), BF16),
            pltpu.VMEM((HID, HID), BF16),
            pltpu.VMEM((STEPS, HID, WIN), F32),
            pltpu.VMEM((4, FEAT, WIN), F32),
            pltpu.VMEM((TAPROWS, HEIGHT * WIN), BF16),
            pltpu.VMEM((TAPROWS, HEIGHT * WIN), F32),
            pltpu.VMEM((2, HID, HEIGHT * WIN), BF16),
            pltpu.VMEM((2, HID, HEIGHT * WIN), BF16),
            pltpu.VMEM((2, HID, CHUNK), F32),
            pltpu.VMEM((HEIGHT, FEAT, WIN), F32),
            pltpu.VMEM((2, ROWS, block), F32),
            pltpu.VMEM((2, ROWS, block), F32),
            pltpu.VMEM((2, ROWS, WIN), F32),
            pltpu.VMEM((2, ROWS, WIN), F32),
            pltpu.VMEM((2, ROWS, block), F32),
            pltpu.VMEM((2, ROWS, block), F32),
            pltpu.VMEM((STEPS, 2, ROWS, block), F32),
            pltpu.VMEM((STEPS, 2, ROWS, block), F32),
            pltpu.VMEM((STEPS, 2, ROWS, block // 2), F32),
            pltpu.VMEM((STEPS, 2, ROWS, block // 2), F32),
            pltpu.VMEM((STEPS, 2, most - 1, ROWS, block // 2), F32),
            pltpu.VMEM((STEPS, 2, most - 1, ROWS, block // 2), F32),
            pltpu.VMEM((STEPS, 1, 1, WIN), F32),
            pltpu.VMEM((STEPS, 1, 1, WIN), F32),
            pltpu.VMEM((STEPS, 1, most - 1, 1, WIN), F32),
            pltpu.VMEM((STEPS, 1, most - 1, 1, WIN), F32),
            dma((7,)),
            dma((7,)),
            dma((STEPS, 2, 2, most - 1)),
            dma((STEPS, 2, 2, most - 1)),
            dma((STEPS, 2, 1, most - 1)),
            dma((STEPS, 2, 1, most - 1)),
        ],
        compiler_params=pltpu.CompilerParams(collective_id=0, has_side_effects=True),
        name="panorama",
    )(
        latent.reshape(32, WIN),
        noise.reshape(STEPS * 32, WIN),
        offsets,
        anchors,
        guidance,
        w_in,
        w_mid,
        w_out,
        t_embed,
        w_feat,
    )
    return out.reshape(2, 4, HALF, WIN).swapaxes(0, 1).reshape(4, HEIGHT, WIN)


def solution(mesh):
    placed = (P("ba", None, "wa"), P(None, "ba", None, "wa"), P("wa"))
    placed += (P(),) * 7
    return jax.shard_map(
        functools.partial(local, mesh.shape["wa"]),
        mesh=mesh,
        in_specs=placed,
        out_specs=P("ba", None, "wa"),
        check_vma=False,
    )
```

time: 240 us -> 74 us (0.31)
  blocking collectives: 130 us -> 0 us
  Pallas kernels: 0 us -> 69.1 us
  matrix products: 29.2 us -> 0 us
  waiting for transfers between devices: 28.9 us -> 0 us
  starting transfers between devices: 16.1 us -> 0 us
  local copies, waits for them, and re-layouts: 16.4 us -> 3.45 us
  between operations: 11.6 us -> 0.67 us
  other arithmetic: 6.67 us -> 0 us
    psum x6 -> x0, blocking collectives: 114 us -> none  [broadcast_by_axis(): shard = lax.psum(shard, axis)]
    pallas_call x0 -> x1, Pallas kernels: none -> 69.1 us  [local(): pl.pallas_call(functools.partial(kernel, count), out_shape=jax.ShapeDtype...]
    dot_general x16 -> x0, matrix products: 29.2 us -> none  [the longest x4 12 us: denoise(): jnp.dot(w_in, stacked, preferred_element_type=jnp.float32)]
    ppermute x5 -> x0, waiting for transfers between devices: 18.3 us -> none  [passed_along(): lax.ppermute(shard, axis, [(i, (i + by) % length) for i in range(length)])]
    all_to_all x1 -> x0, blocking collectives: 15.8 us -> none  [from_everyone(): return lax.all_to_all(copies, axis, split_axis=0, concat_axis=0, tiled=True)]
    ppermute x5 -> x0, starting transfers between devices: 11.3 us -> none  [passed_along(): lax.ppermute(shard, axis, [(i, (i + by) % length) for i in range(length)])]
    all_to_all x1 -> x0, waiting for transfers between devices: 10.6 us -> none  [from_everyone(): return lax.all_to_all(copies, axis, split_axis=0, concat_axis=0, tiled=True)]
    dynamic_update_slice x4 -> x0, local copies, waits for them, and re-layouts: 5.25 us -> none  [window_update(): lax.dynamic_update_slice_in_dim(summed, current + advanced[index], starts...]
  transfers between devices with their start and end apart: 6 -> 0, of which waited for: 4 -> 0; matrix products, arithmetic and copies ran while one was open for 12% -> 0% of each run, Pallas kernels for 0% -> 0%
where the time goes in v1:
time: 74 us; the launch traced here: 73.2 us
  Pallas kernels  69.1 us (93%)
  local copies, waits for them, and re-layouts  3.45 us (5%)
    pallas_call x1, Pallas kernels, local(): pl.pallas_call(functools.partial(kernel, count), out_shape=jax.ShapeDtype...  69.1 us
    unnamed x4, local copies, waits for them, and re-layouts  2.11 us

profile of v1, /device:TPU:2, one launch (start us, length us, event | category | flops | bytes accessed | tf_op | source)
XLA Modules:
  0.0 73.2 jit_solution(14810329344888112541)
XLA Ops:
  0.0 0.0 copy-start
  0.7 1.4 %copy.12.w_feat_ref = f32[64,4]{1,0:T(8,128)} copy(f32[64,4]{0,1:T(4,128)} %param.19) | data formatting | bytes 2048 | tf_op args[9]
  2.0 0.0 copy-done
  2.0 0.7 %copy.11.w_in_ref = bf16[320,36]{1,0:T(8,128)(2,1)} copy(bf16[320,36]{0,1:T(8,128)(2,1)S(1)} %copy-done) | data formatting | bytes 46080 | tf_op args[5]
  2.8 69.1 %panorama.1 = f32[8,512]{1,0:T(8,128)} custom-call(f32[32,128]{1,0:T(8,128)} %bitcast.6, f32[64,128]{1,0:T(8,128)} %bitcast.5, s32[2]{0:T(128)} %offsets_ref.1, s32[2]{0:T(128)} %anchors_ref.1, f32[1]{0:T(128)S(6)} %copy.14.guidance_ref, bf16[320,36]{1,0:T(8,128)(2,1)} %copy.11.w_in_ref, bf16[320,320]{1,0:T(8,128)(2,1)} %w_mid_ref.1, ...), custom_call_target="tpu_custom_call" | custom-call | tf_op jit(solution)/shard_map/panorama/pallas_call | solution.py:524
  71.9 0.7 reshape.14
  72.6 0.6 copy.13
Async XLA Ops:
  0.0 2.0 %copy-start = (bf16[320,36]{0,1:T(8,128)(2,1)S(1)}, bf16[320,36]{0,1:T(8,128)(2,1)}, u32[]{:S(2)}) copy-start(bf16[320,36]{0,1:T(8,128)(2,1)} %param.15) | copy-start | bytes 69124

commit v2 on v1

v2 whole, which is shorter than its diff:
```python
import functools
import math

import jax
import jax.numpy as jnp
from jax import lax
from jax.experimental import pallas as pl
from jax.experimental.pallas import tpu as pltpu
from jax.sharding import PartitionSpec as P

WIN = 128
STRIDE = 64
STEPS = 2
ROWS = 8
HEIGHT = 8
HALF = 4
HID = 320
FEAT = 64
TAPROWS = 80
CHUNK = 256
MESH = pl.DeviceIdType.MESH
F32 = jnp.float32
BF16 = jnp.bfloat16

TAP_SHIFTS = ((-1, -1), (-1, 0), (-1, 1), (0, -1), (0, 0), (0, 1), (1, -1), (1, 0), (1, 1))
CUMULATIVE_ALPHA = (0.35, 0.55, 0.72, 0.85, 0.93)
STABILITY = 1e-06


def plan(number):
    current = CUMULATIVE_ALPHA[number]
    following = CUMULATIVE_ALPHA[number + 1]
    spread = 0.3 * math.sqrt(1.0 - following)
    return (
        math.sqrt(current),
        math.sqrt(1.0 - current),
        math.sqrt(following),
        math.sqrt(1.0 - following - spread * spread),
        spread,
    )


def group_sizes(count):
    inner = 8 if count % 8 == 0 else 2
    return inner, count // inner


def lane_iota():
    return lax.broadcasted_iota(jnp.int32, (ROWS, WIN), 1)


def row_iota():
    return lax.broadcasted_iota(jnp.int32, (ROWS, WIN), 0)


def sideways(tile, by):
    if by == 0:
        return tile
    lanes = lane_iota()
    if by == 1:
        return jnp.where(lanes < WIN - 1, pltpu.roll(tile, WIN - 1, 1), 0.0)
    return jnp.where(lanes > 0, pltpu.roll(tile, 1, 1), 0.0)


def swapped(tile):
    return pltpu.roll(tile, 4, 0)


def low_high(low, high):
    return jnp.where(row_iota() < 4, low, high)


def store_taps(ref, tiles, sign):
    by_shift = {by: [sideways(tile, by) for tile in tiles] for by in (-1, 0, 1)}
    zero = jnp.zeros((ROWS, WIN), F32)

    def piece(k, h):
        if k >= len(TAP_SHIFTS):
            return zero
        down_by, right_by = TAP_SHIFTS[k]
        at = h + sign * down_by
        if at < 0 or at >= HEIGHT:
            return zero
        return by_shift[sign * right_by][at]

    for h in range(HEIGHT):
        for pair in range(TAPROWS // 16):
            both = jnp.concatenate([piece(2 * pair, h), piece(2 * pair + 1, h)], axis=0)
            ref[16 * pair : 16 * pair + 16, h * WIN : (h + 1) * WIN] = both.astype(BF16)


def summed_taps(ref, sign, rounded):
    tiles = []
    for h in range(HEIGHT):
        by_shift = {}
        for k, (down_by, right_by) in enumerate(TAP_SHIFTS):
            at = h + sign * down_by
            if at < 0 or at >= HEIGHT:
                continue
            value = ref[8 * k : 8 * k + 8, at * WIN : (at + 1) * WIN]
            if rounded:
                value = value.astype(BF16).astype(F32)
            shift = sign * right_by
            by_shift[shift] = value if shift not in by_shift else by_shift[shift] + value
        tiles.append(
            by_shift[0] + sideways(by_shift[-1], -1) + sideways(by_shift[1], 1)
        )
    return tiles


def gate_of(value):
    return 0.5 * jnp.tanh(0.5 * value) + 0.5


def dot(left, right):
    return jnp.dot(left, right, preferred_element_type=F32)


def dot_nt(left, right):
    return lax.dot_general(
        left, right, (((1,), (1,)), ((), ())), preferred_element_type=F32
    )


def kernel(
    count,
    latent_ref,
    noise_ref,
    offsets_ref,
    anchors_ref,
    guidance_ref,
    w_in_ref,
    w_mid_ref,
    w_out_ref,
    t_embed_ref,
    w_feat_ref,
    out_ref,
    win_ref,
    wint_ref,
    wout_ref,
    woutt_ref,
    wmidt_ref,
    embed_ref,
    feat_ref,
    taps_ref,
    outward_ref,
    d1_ref,
    d2_ref,
    percept_ref,
    halo_src,
    halo_dst,
    cover_src,
    cover_dst,
    sums_left_src,
    sums_left_dst,
    sums_right_src,
    sums_right_dst,
    casts_a,
    casts_b,
    firsts_a,
    firsts_b,
    seconds_a,
    seconds_b,
    square_src,
    square_mid,
    square_first,
    square_second,
    edge_send,
    edge_recv,
    cast_send,
    cast_recv,
    square_send,
    square_recv,
):
    inner, outer = group_sizes(count)
    me = lax.axis_index("wa")
    part = lax.axis_index("ba")
    my_inner = lax.rem(me, inner)
    my_outer = me // inner
    right = lax.rem(me + 1, count)
    left = lax.rem(me + count - 1, count)

    def inner_peer(by):
        return my_outer * inner + lax.rem(my_inner + by, inner)

    def outer_peer(by):
        return lax.rem(my_outer + by, outer) * inner + my_inner

    barrier = pltpu.get_barrier_semaphore()
    peers = [inner_peer(by) for by in range(1, inner)]
    peers += [outer_peer(by) for by in range(1, outer)]
    peers += [left, right]
    for peer in peers:
        pl.semaphore_signal(barrier, inc=1, device_id=(peer, part), device_id_type=MESH)

    def remote(source, target, send, recv, peer):
        return pltpu.make_async_remote_copy(
            src_ref=source,
            dst_ref=target,
            send_sem=send,
            recv_sem=recv,
            device_id=(peer, part),
            device_id_type=MESH,
        )

    lanes = lane_iota()
    starts = [slot * STRIDE + offsets_ref[slot] for slot in range(2)]
    owners = [anchors_ref[number] // 2 for number in range(STEPS)]
    slots_of = [anchors_ref[number] - 2 * owner for number, owner in enumerate(owners)]

    def flag(condition):
        return jnp.where(condition, 1.0, 0.0)

    def packed(ref, base):
        return [
            jnp.concatenate(
                [
                    ref[pl.ds(base + tile, 4, stride=8), :],
                    ref[pl.ds(base + tile + HALF, 4, stride=8), :],
                ],
                axis=0,
            )
            for tile in range(HALF)
        ]

    def put(ref, index, tiles):
        for tile, value in enumerate(tiles):
            ref[(*index, slice(None), slice(tile * WIN, (tile + 1) * WIN))] = value

    def got(ref, *index, size=HALF):
        return [ref[(*index, slice(None), slice(t * WIN, (t + 1) * WIN))] for t in range(size)]

    own = packed(latent_ref, 0)
    noise = [packed(noise_ref, 32 * number) for number in range(STEPS)]
    put(halo_src, (0,), own)
    put(halo_src, (1,), noise[0])
    cover_own = sum(flag(lanes >= start) for start in starts)
    cover_next = sum(flag(lanes < start) for start in starts)
    cover_src[0] = cover_own
    cover_src[1] = cover_next

    shares = []
    for number in range(STEPS):
        mine = [flag(anchors_ref[number] == 2 * me + slot) for slot in range(2)]
        shares.append(
            mine[0] * offsets_ref[0].astype(F32) + mine[1] * offsets_ref[1].astype(F32)
        )
    is_first = flag(owners[0] == me)
    is_second = flag(owners[0] == left)
    put(casts_a, (0, 0), [tile * is_first for tile in own])
    casts_a[0, 0, :, HALF * WIN :] = jnp.where(row_iota() < 4, shares[0], shares[1])
    put(casts_b, (0, 0), [tile * is_second for tile in own])

    def one_hot(slot):
        wide = lax.broadcasted_iota(jnp.int32, (TAPROWS, 36), 0)
        small = lax.broadcasted_iota(jnp.int32, (TAPROWS, 36), 1)
        tap = small // 4
        return flag(wide == tap * 8 + slot * 4 + (small - tap * 4)).astype(BF16)

    eye = flag(
        lax.broadcasted_iota(jnp.int32, (HID, HID), 0)
        == lax.broadcasted_iota(jnp.int32, (HID, HID), 1)
    )
    eye_b = eye.astype(BF16)
    w_in = w_in_ref[...]
    w_out = w_out_ref[...]
    for slot in range(2):
        spread_rows = one_hot(slot)
        wint = dot(spread_rows, w_in).astype(BF16)
        wint_ref[slot] = wint
        win_ref[slot] = dot_nt(eye_b, wint).astype(BF16)
        wout = dot(spread_rows, w_out).astype(BF16)
        wout_ref[slot] = wout
        woutt_ref[slot] = dot_nt(eye_b, wout).astype(BF16)
    wmidt_ref[...] = dot_nt(eye_b, w_mid_ref[...]).astype(BF16)
    for number in range(STEPS):
        column = jnp.sum(eye * t_embed_ref[number : number + 1, :], axis=1, keepdims=True)
        embed_ref[number] = jnp.broadcast_to(column, (HID, WIN))
    for channel in range(4):
        column = jnp.sum(
            eye[:FEAT, :FEAT] * w_feat_ref[channel : channel + 1, :], axis=1, keepdims=True
        )
        feat_ref[channel] = jnp.broadcast_to(column, (FEAT, WIN))

    def denoised(tiles, number, slots, keep):
        store_taps(taps_ref, tiles, 1)
        embedding = jnp.concatenate([embed_ref[number]] * (CHUNK // WIN), axis=1)
        for step in range(HEIGHT * WIN // CHUNK):
            at = slice(step * CHUNK, (step + 1) * CHUNK)
            total = None
            for slot in slots:
                hidden = dot(win_ref[slot], taps_ref[:, at]) + embedding
                gate = gate_of(hidden)
                active = hidden * gate
                if keep:
                    d1_ref[slot, :, at] = (gate + active * (1.0 - gate)).astype(BF16)
                middle = dot(w_mid_ref[...], active.astype(BF16))
                gate = gate_of(middle)
                active = middle * gate
                if keep:
                    d2_ref[slot, :, at] = (gate + active * (1.0 - gate)).astype(BF16)
                joined = (hidden + active).astype(BF16)
                outward = dot(wout_ref[slot], joined)
                total = outward if total is None else total + outward
            outward_ref[:, at] = total
        return summed_taps(outward_ref, 1, False)

    def pulled_back(tiles):
        store_taps(taps_ref, tiles, -1)
        for step in range(HEIGHT * WIN // CHUNK):
            at = slice(step * CHUNK, (step + 1) * CHUNK)
            total = None
            for slot in range(2):
                joined = dot(woutt_ref[slot], taps_ref[:, at]).astype(BF16).astype(F32)
                middle = (joined * d2_ref[slot, :, at].astype(F32)).astype(BF16)
                active = dot(wmidt_ref[...], middle).astype(BF16).astype(F32)
                hidden = (joined + active * d1_ref[slot, :, at].astype(F32)).astype(BF16)
                inward = dot(wint_ref[slot], hidden)
                total = inward if total is None else total + inward
            outward_ref[:, at] = total
        return summed_taps(outward_ref, -1, True)

    def features(tile, slot):
        total = None
        for channel in range(4):
            row = tile[slot * 4 + channel : slot * 4 + channel + 1, :]
            term = feat_ref[channel] * row
            total = term if total is None else total + term
        return total

    def cut(first, second, start):
        back = lax.rem(WIN - start, WIN)
        return [
            jnp.where(
                lanes < WIN - start,
                pltpu.roll(first[tile], back, 1),
                pltpu.roll(second[tile], back, 1),
            )
            for tile in range(HALF)
        ]

    def windows_of(first, second):
        both = [cut(first, second, start) for start in starts]
        tiles = [low_high(both[0][tile], swapped(both[1][tile])) for tile in range(HALF)]
        tiles += [low_high(swapped(both[0][tile]), both[1][tile]) for tile in range(HALF)]
        return tiles

    def pieces_of(tiles):
        lows, highs = tiles[:HALF], tiles[HALF:]
        return (
            [low_high(low, swapped(high)) for low, high in zip(lows, highs)],
            [low_high(swapped(low), high) for low, high in zip(lows, highs)],
        )

    def placed(pieces):
        turned = [
            [pltpu.roll(tile, start, 1) for tile in piece]
            for piece, start in zip(pieces, starts)
        ]
        pairs = list(zip(*turned))
        own_sum = [
            sum(jnp.where(lanes >= start, t, 0.0) for t, start in zip(pair, starts))
            for pair in pairs
        ]
        next_sum = [
            sum(jnp.where(lanes < start, t, 0.0) for t, start in zip(pair, starts))
            for pair in pairs
        ]
        return own_sum, next_sum

    def far_first(size):
        return sorted(range(1, size), key=lambda by: -min(by, size - by))

    def exchange(along_inner, source, target, send, recv):
        started = []
        for by in far_first(inner if along_inner else outer):
            peer = inner_peer(by) if along_inner else outer_peer(by)
            copy = remote(source, target.at[by - 1], send.at[by - 1], recv.at[by - 1], peer)
            copy.start()
            started.append((by, copy))
        return started

    def finish(started, source, target):
        total = source[...]
        for by, copy in started:
            copy.wait_recv()
            total = total + target[by - 1]
        return total

    sent = []

    def cast_start(number):
        return [
            exchange(
                half == 0,
                (casts_a, casts_b)[half].at[number, 0],
                (firsts_a, firsts_b)[half].at[number],
                cast_send.at[number, 0, half],
                cast_recv.at[number, 0, half],
            )
            for half in range(2)
        ]

    def cast_middle(number, started):
        out = []
        for half in range(2):
            source = (casts_a, casts_b)[half].at[number]
            source[1] = finish(started[half], source.at[0], (firsts_a, firsts_b)[half].at[number])
            out.append(
                exchange(
                    half == 1,
                    source.at[1],
                    (seconds_a, seconds_b)[half].at[number],
                    cast_send.at[number, 1, half],
                    cast_recv.at[number, 1, half],
                )
            )
            sent.extend(started[half])
        return out

    def cast_end(number, started):
        out = []
        for half in range(2):
            source = (casts_a, casts_b)[half].at[number, 1]
            total = finish(started[half], source, (seconds_a, seconds_b)[half].at[number])
            out.append([total[:, t * WIN : (t + 1) * WIN] for t in range(total.shape[1] // WIN)])
            sent.extend(started[half])
        return out

    pl.semaphore_wait(barrier, len(peers))

    started = cast_start(0)
    copies = [
        remote(halo_src.at[0], halo_dst.at[0], edge_send.at[0], edge_recv.at[0], left),
        remote(cover_src.at[0], cover_dst.at[0], edge_send.at[2], edge_recv.at[2], left),
        remote(cover_src.at[1], cover_dst.at[1], edge_send.at[3], edge_recv.at[3], right),
        remote(halo_src.at[1], halo_dst.at[1], edge_send.at[1], edge_recv.at[1], left),
    ]
    for copy in copies:
        copy.start()
        sent.append((0, copy))
    started = cast_middle(0, started)
    copies[0].wait_recv()
    following = got(halo_dst, 0)

    for number in range(STEPS):
        now_a, now_s, next_a, direction, spread = plan(number)
        last = number == STEPS - 1
        tiles = windows_of(own, following)
        predicted = denoised(tiles, number, (0, 1), True)
        cleaned = [(x - now_s * p) * (1.0 / now_a) for x, p in zip(tiles, predicted)]
        base = pieces_of(
            [(next_a / now_a) * (x - now_s * p) + direction * p for x, p in zip(tiles, predicted)]
        )
        base_own, base_next = placed(base)
        if number == 0:
            for copy in copies[1:]:
                copy.wait_recv()
            count_own = cover_own + cover_dst[1]
            per_own = 1.0 / count_own
            per_next = 1.0 / (cover_next + cover_dst[0])
            noise_next = got(halo_dst, 1)

        totals = cast_end(number, started)
        if number == 0:
            anchor_starts = [
                slots_of[step] * STRIDE
                + jnp.max(totals[0][HALF][4 * step : 4 * step + 1, :]).astype(jnp.int32)
                for step in range(STEPS)
            ]
            picked = cut(totals[0][:HALF], totals[1], anchor_starts[0])
        else:
            factor = 1.0 / totals[0][HALF]
            picked = [
                (totals[t // 2][t % 2] - scale * totals[t // 2][2 + t % 2]) * factor
                for t in range(HALF)
            ]
        anchor_tiles = picked + [swapped(tile) for tile in picked]
        anchor_predicted = denoised(anchor_tiles, number, (0,), False)
        for h in range(HEIGHT):
            clean = (anchor_tiles[h] - now_s * anchor_predicted[h]) * (1.0 / now_a)
            value = features(clean, 0)
            percept_ref[h] = value * gate_of(value)

        clean_grad = []
        for h in range(HEIGHT):
            grad = jnp.zeros((ROWS, WIN), F32)
            for slot in range(2):
                value = features(cleaned[h], slot)
                gate = gate_of(value)
                active = value * gate
                slope = gate + active * (1.0 - gate)
                pull = (active - percept_ref[h]) * slope * (1.0 / FEAT)
                for channel in range(4):
                    row = jnp.sum(feat_ref[channel] * pull, axis=0, keepdims=True)
                    grad = jnp.where(row_iota() == slot * 4 + channel, row, grad)
            clean_grad.append(grad)
        pulled = pulled_back([(-now_s / now_a) * grad for grad in clean_grad])
        gradient = [p + g * (1.0 / now_a) for p, g in zip(pulled, clean_grad)]

        squares = sum(g * g for g in gradient)
        square = jnp.sum(jnp.sum(squares, axis=1, keepdims=True), axis=0, keepdims=True)
        square_src[number] = jnp.broadcast_to(square, (1, WIN))
        first = exchange(
            True,
            square_src.at[number],
            square_first.at[number],
            square_send.at[number, 0],
            square_recv.at[number, 0],
        )

        grads = pieces_of(gradient)
        if not last:
            width = count * WIN
            origin = owners[1] * WIN + anchor_starts[1]

            def apart(column):
                return lax.rem(column - origin + width + width // 2, width) - width // 2

            def framed(packed_tiles, by):
                turn = lax.rem(by + width, WIN)
                inside = (lanes >= by) & (lanes < by + WIN)
                return [jnp.where(inside, pltpu.roll(t, turn, 1), 0.0) for t in packed_tiles]

            gaps = [apart(me * WIN + start) for start in starts]
            parts = [framed(piece, gap) for piece, gap in zip(base, gaps)]
            parts.append(framed([spread * n * count_own for n in noise[0]], apart(me * WIN)))
            base_part = [a + b + c for a, b, c in zip(*parts)]
            grad_part = [
                a + b for a, b in zip(*[framed(piece, gap) for piece, gap in zip(grads, gaps)])
            ]
            cover = sum(flag((lanes >= gap) & (lanes < gap + WIN)) for gap in gaps)
            put(casts_a, (1, 0), base_part[:2] + grad_part[:2] + [cover])
            put(casts_b, (1, 0), base_part[2:] + grad_part[2:])
            started = cast_start(1)

        grad_own, grad_next = placed(grads)
        put(sums_right_src, (number, 0), base_next)
        put(sums_right_src, (number, 1), grad_next)
        to_right = remote(
            sums_right_src.at[number],
            sums_right_dst.at[number],
            edge_send.at[4 + number],
            edge_recv.at[4 + number],
            right,
        )
        to_right.start()
        sent.append((0, to_right))
        if not last:
            put(sums_left_src, (0,), base_own)
            put(sums_left_src, (1,), grad_own)
            to_left = remote(
                sums_left_src, sums_left_dst, edge_send.at[6], edge_recv.at[6], left
            )
            to_left.start()
            sent.append((0, to_left))

        square_mid[number] = finish(first, square_src.at[number], square_first.at[number])
        second = exchange(
            False,
            square_mid.at[number],
            square_second.at[number],
            square_send.at[number, 1],
            square_recv.at[number, 1],
        )
        sent += first + second
        if not last:
            started = cast_middle(1, started)
        to_right.wait_recv()
        base_in = got(sums_right_dst, number, 0)
        grad_in = got(sums_right_dst, number, 1)
        if not last:
            to_left.wait_recv()
            base_far = got(sums_left_dst, 0)
            grad_far = got(sums_left_dst, 1)
        total = finish(second, square_mid.at[number], square_second.at[number])
        entries = 2 * count * 4 * HEIGHT * WIN
        scale = guidance_ref[0] * lax.rsqrt(total * (1.0 / entries) + STABILITY)
        scale = (next_a / now_a) * scale
        own = [
            (base_own[t] + base_in[t] - scale * (grad_own[t] + grad_in[t])) * per_own
            + spread * noise[number][t]
            for t in range(HALF)
        ]
        if not last:
            following = [
                (base_next[t] + base_far[t] - scale * (grad_next[t] + grad_far[t])) * per_next
                + spread * noise_next[t]
                for t in range(HALF)
            ]

    for tile in range(HALF):
        out_ref[pl.ds(tile, 4, stride=8), :] = own[tile][:4]
        out_ref[pl.ds(tile + HALF, 4, stride=8), :] = own[tile][4:]
    for _, copy in sent:
        copy.wait_send()


def local(count, latent, noise, offsets, anchors, guidance, w_in, w_mid, w_out, t_embed, w_feat):
    inner, outer = group_sizes(count)
    most = max(inner, outer)
    vmem = pl.BlockSpec(memory_space=pltpu.VMEM)
    smem = pl.BlockSpec(memory_space=pltpu.SMEM)
    block = HALF * WIN
    dma = pltpu.SemaphoreType.DMA
    out = pl.pallas_call(
        functools.partial(kernel, count),
        out_shape=jax.ShapeDtypeStruct((32, WIN), F32),
        in_specs=[vmem, vmem, smem, smem, smem, vmem, vmem, vmem, vmem, vmem],
        out_specs=vmem,
        scratch_shapes=[
            pltpu.VMEM((2, HID, TAPROWS), BF16),
            pltpu.VMEM((2, TAPROWS, HID), BF16),
            pltpu.VMEM((2, TAPROWS, HID), BF16),
            pltpu.VMEM((2, HID, TAPROWS), BF16),
            pltpu.VMEM((HID, HID), BF16),
            pltpu.VMEM((STEPS, HID, WIN), F32),
            pltpu.VMEM((4, FEAT, WIN), F32),
            pltpu.VMEM((TAPROWS, HEIGHT * WIN), BF16),
            pltpu.VMEM((TAPROWS, HEIGHT * WIN), F32),
            pltpu.VMEM((2, HID, HEIGHT * WIN), BF16),
            pltpu.VMEM((2, HID, HEIGHT * WIN), BF16),
            pltpu.VMEM((HEIGHT, FEAT, WIN), F32),
            pltpu.VMEM((2, ROWS, block), F32),
            pltpu.VMEM((2, ROWS, block), F32),
            pltpu.VMEM((2, ROWS, WIN), F32),
            pltpu.VMEM((2, ROWS, WIN), F32),
            pltpu.VMEM((2, ROWS, block), F32),
            pltpu.VMEM((2, ROWS, block), F32),
            pltpu.VMEM((STEPS, 2, ROWS, block), F32),
            pltpu.VMEM((STEPS, 2, ROWS, block), F32),
            pltpu.VMEM((STEPS, 2, ROWS, block + WIN), F32),
            pltpu.VMEM((STEPS, 2, ROWS, block), F32),
            pltpu.VMEM((STEPS, inner - 1, ROWS, block + WIN), F32),
            pltpu.VMEM((STEPS, outer - 1, ROWS, block), F32),
            pltpu.VMEM((STEPS, outer - 1, ROWS, block + WIN), F32),
            pltpu.VMEM((STEPS, inner - 1, ROWS, block), F32),
            pltpu.VMEM((STEPS, 1, WIN), F32),
            pltpu.VMEM((STEPS, 1, WIN), F32),
            pltpu.VMEM((STEPS, inner - 1, 1, WIN), F32),
            pltpu.VMEM((STEPS, outer - 1, 1, WIN), F32),
            dma((7,)),
            dma((7,)),
            dma((STEPS, 2, 2, most - 1)),
            dma((STEPS, 2, 2, most - 1)),
            dma((STEPS, 2, most - 1)),
            dma((STEPS, 2, most - 1)),
        ],
        compiler_params=pltpu.CompilerParams(collective_id=0, has_side_effects=True),
        name="panorama",
    )(
        latent.reshape(32, WIN),
        noise.reshape(STEPS * 32, WIN),
        offsets,
        anchors,
        guidance,
        w_in.T,
        w_mid,
        w_out,
        t_embed,
        w_feat.T,
    )
    return out.reshape(4, HEIGHT, WIN)


def solution(mesh):
    placed = (P("ba", None, "wa"), P(None, "ba", None, "wa"), P("wa"))
    placed += (P(),) * 7
    return jax.shard_map(
        functools.partial(local, mesh.shape["wa"]),
        mesh=mesh,
        in_specs=placed,
        out_specs=P("ba", None, "wa"),
        check_vma=False,
    )
```

time: 74 us -> 58.4 us (0.79)
  Pallas kernels: 69.1 us -> 56.2 us
  local copies, waits for them, and re-layouts: 3.45 us -> 1.32 us
    pallas_call x1, Pallas kernels: 69.1 us -> 56.2 us  [local(): pl.pallas_call(functools.partial(kernel, count), out_shape=jax.ShapeDtype...]
    unnamed x4 -> x1, local copies, waits for them, and re-layouts: 2.11 us -> 1.32 us
where the time goes in v2:
time: 58.4 us; the launch traced here: 58.2 us
  Pallas kernels  56.2 us (96%)
  local copies, waits for them, and re-layouts  1.32 us (2%)
  between operations  0.66 us (1%)
    pallas_call x1, Pallas kernels, local(): pl.pallas_call(functools.partial(kernel, count), out_shape=jax.ShapeDtype...  56.2 us
    unnamed x1, local copies, waits for them, and re-layouts  1.32 us

profile of v2, /device:TPU:2, one launch (start us, length us, event | category | flops | bytes accessed | tf_op | source)
XLA Modules:
  0.0 58.2 jit_solution(10937268410767963026)
XLA Ops:
  0.7 56.2 %panorama.1 = f32[32,128]{1,0:T(8,128)} custom-call(f32[32,128]{1,0:T(8,128)} %bitcast.8, f32[64,128]{1,0:T(8,128)} %bitcast.6, s32[2]{0:T(128)} %offsets_ref.1, s32[2]{0:T(128)} %anchors_ref.1, f32[1]{0:T(128)S(6)} %copy.12.guidance_ref, bf16[36,320]{1,0:T(8,128)(2,1)} %bitcast.7, bf16[320,320]{1,0:T(8,128)(2,1)} %w_mid_ref.1, bf16[36,320]{1,0:T(8,128)(2,1)} %w_out_ref.1, ...), custom_call_target="tpu_custom_call" | custom-call | tf_op jit(solution)/shard_map/panorama/pallas_call | solution.py:606
  56.8 1.3 %copy.13 = f32[4,8,128]{2,1,0:T(8,128)} copy(f32[4,8,128]{2,1,0:T(8,128)} %bitcast.5) | data formatting | bytes 32768

commit v3 on v2

--- a/solution.py
+++ b/solution.py
@@ -17,7 +17,8 @@
 HID = 320
 FEAT = 64
 TAPROWS = 80
-CHUNK = 256
+ONES = 72
+CHUNK = 512
 MESH = pl.DeviceIdType.MESH
 F32 = jnp.float32
 BF16 = jnp.bfloat16
@@ -73,10 +74,11 @@
 def store_taps(ref, tiles, sign):
     by_shift = {by: [sideways(tile, by) for tile in tiles] for by in (-1, 0, 1)}
     zero = jnp.zeros((ROWS, WIN), F32)
+    one = jnp.ones((ROWS, WIN), F32)
 
     def piece(k, h):
         if k >= len(TAP_SHIFTS):
-            return zero
+            return one
         down_by, right_by = TAP_SHIFTS[k]
         at = h + sign * down_by
         if at < 0 or at >= HEIGHT:
@@ -112,6 +114,13 @@
     return 0.5 * jnp.tanh(0.5 * value) + 0.5
 
 
+def silu_of_half(half):
+    turn = jnp.tanh(half)
+    gate = turn + 1.0
+    active = half * gate
+    return active, gate + active * (1.0 - turn)
+
+
 def dot(left, right):
     return jnp.dot(left, right, preferred_element_type=F32)
 
@@ -122,8 +131,26 @@
     )
 
 
+def in_turn(units, stages, apart):
+    for step in range(len(units) + apart * (len(stages) - 1)):
+        for late, stage in enumerate(stages):
+            if 0 <= step - late * apart < len(units):
+                stage(*units[step - late * apart])
+
+
 def kernel(
     count,
+    latent_hbm,
+    noise_hbm,
+    offsets_hbm,
+    anchors_hbm,
+    guidance_hbm,
+    w_in_hbm,
+    w_mid_hbm,
+    w_out_hbm,
+    t_embed_hbm,
+    w_feat_hbm,
+    out_ref,
     latent_ref,
     noise_ref,
     offsets_ref,
@@ -134,13 +161,12 @@
     w_out_ref,
     t_embed_ref,
     w_feat_ref,
-    out_ref,
     win_ref,
     wint_ref,
     wout_ref,
     woutt_ref,
+    wmid_ref,
     wmidt_ref,
-    embed_ref,
     feat_ref,
     taps_ref,
     outward_ref,
@@ -171,6 +197,7 @@
     cast_recv,
     square_send,
     square_recv,
+    load_sem,
 ):
     inner, outer = group_sizes(count)
     me = lax.axis_index("wa")
@@ -193,6 +220,30 @@
     for peer in peers:
         pl.semaphore_signal(barrier, inc=1, device_id=(peer, part), device_id_type=MESH)
 
+    pairs = [
+        (offsets_hbm, offsets_ref),
+        (anchors_hbm, anchors_ref),
+        (latent_hbm, latent_ref),
+        (noise_hbm, noise_ref),
+        (w_in_hbm, w_in_ref),
+        (w_mid_hbm, w_mid_ref),
+        (w_out_hbm, w_out_ref),
+        (t_embed_hbm, t_embed_ref),
+        (w_feat_hbm, w_feat_ref),
+        (guidance_hbm, guidance_ref),
+    ]
+    loads = [
+        pltpu.make_async_copy(source, target, load_sem.at[index])
+        for index, (source, target) in enumerate(pairs)
+    ]
+    for load in loads:
+        load.start()
+    first_loads, weights = loads[:4], loads[4:]
+
+    def arrive(some):
+        for load in some:
+            load.wait()
+
     def remote(source, target, send, recv, peer):
         return pltpu.make_async_remote_copy(
             src_ref=source,
@@ -203,6 +254,7 @@
             device_id_type=MESH,
         )
 
+    arrive(first_loads)
     lanes = lane_iota()
     starts = [slot * STRIDE + offsets_ref[slot] for slot in range(2)]
     owners = [anchors_ref[number] // 2 for number in range(STEPS)]
@@ -262,20 +314,27 @@
         == lax.broadcasted_iota(jnp.int32, (HID, HID), 1)
     )
     eye_b = eye.astype(BF16)
+    arrive(weights)
     w_in = w_in_ref[...]
     w_out = w_out_ref[...]
+    tap_rows = lax.broadcasted_iota(jnp.int32, (TAPROWS, HID), 0)
     for slot in range(2):
         spread_rows = one_hot(slot)
-        wint = dot(spread_rows, w_in).astype(BF16)
-        wint_ref[slot] = wint
-        win_ref[slot] = dot_nt(eye_b, wint).astype(BF16)
+        wint = 0.5 * dot(spread_rows, w_in)
+        wint_ref[slot] = wint.astype(BF16)
+        for number in range(STEPS):
+            rest = 0.5 * t_embed_ref[number : number + 1, :]
+            full = wint
+            for level in range(3):
+                level_part = rest.astype(BF16).astype(F32)
+                rest = rest - level_part
+                full = jnp.where(tap_rows == ONES + level, level_part, full)
+            win_ref[number, slot] = dot_nt(eye_b, full.astype(BF16)).astype(BF16)
         wout = dot(spread_rows, w_out).astype(BF16)
         wout_ref[slot] = wout
         woutt_ref[slot] = dot_nt(eye_b, wout).astype(BF16)
-    wmidt_ref[...] = dot_nt(eye_b, w_mid_ref[...]).astype(BF16)
-    for number in range(STEPS):
-        column = jnp.sum(eye * t_embed_ref[number : number + 1, :], axis=1, keepdims=True)
-        embed_ref[number] = jnp.broadcast_to(column, (HID, WIN))
+    wmid_ref[...] = (0.5 * w_mid_ref[...].astype(F32)).astype(BF16)
+    wmidt_ref[...] = (0.25 * dot_nt(eye_b, w_mid_ref[...])).astype(BF16)
     for channel in range(4):
         column = jnp.sum(
             eye[:FEAT, :FEAT] * w_feat_ref[channel : channel + 1, :], axis=1, keepdims=True
@@ -284,41 +343,60 @@
 
     def denoised(tiles, number, slots, keep):
         store_taps(taps_ref, tiles, 1)
-        embedding = jnp.concatenate([embed_ref[number]] * (CHUNK // WIN), axis=1)
-        for step in range(HEIGHT * WIN // CHUNK):
+        units = [(step, slot) for step in range(HEIGHT * WIN // CHUNK) for slot in slots]
+        held, totals = {}, {}
+
+        def stage_in(step, slot):
             at = slice(step * CHUNK, (step + 1) * CHUNK)
-            total = None
-            for slot in slots:
-                hidden = dot(win_ref[slot], taps_ref[:, at]) + embedding
-                gate = gate_of(hidden)
-                active = hidden * gate
-                if keep:
-                    d1_ref[slot, :, at] = (gate + active * (1.0 - gate)).astype(BF16)
-                middle = dot(w_mid_ref[...], active.astype(BF16))
-                gate = gate_of(middle)
-                active = middle * gate
-                if keep:
-                    d2_ref[slot, :, at] = (gate + active * (1.0 - gate)).astype(BF16)
-                joined = (hidden + active).astype(BF16)
-                outward = dot(wout_ref[slot], joined)
-                total = outward if total is None else total + outward
-            outward_ref[:, at] = total
+            hidden = dot(win_ref[number, slot], taps_ref[:, at])
+            half = hidden.astype(BF16)
+            active, slope = silu_of_half(half)
+            if keep:
+                d1_ref[slot, :, at] = slope
+            held[step, slot] = (hidden, active)
+
+        def stage_mid(step, slot):
+            at = slice(step * CHUNK, (step + 1) * CHUNK)
+            hidden, active = held[step, slot]
+            middle = dot(wmid_ref[...], active)
+            active, slope = silu_of_half(middle.astype(BF16))
+            if keep:
+                d2_ref[slot, :, at] = slope
+            held[step, slot] = (hidden + hidden + active.astype(F32)).astype(BF16)
+
+        def stage_out(step, slot):
+            outward = dot(wout_ref[slot], held[step, slot])
+            totals[step] = totals[step] + outward if step in totals else outward
+            if slot == slots[-1]:
+                outward_ref[:, step * CHUNK : (step + 1) * CHUNK] = totals[step]
+
+        in_turn(units, (stage_in, stage_mid, stage_out), 2)
         return summed_taps(outward_ref, 1, False)
 
     def pulled_back(tiles):
         store_taps(taps_ref, tiles, -1)
-        for step in range(HEIGHT * WIN // CHUNK):
+        units = [(step, slot) for step in range(HEIGHT * WIN // CHUNK) for slot in range(2)]
+        held, totals = {}, {}
+
+        def stage_out(step, slot):
             at = slice(step * CHUNK, (step + 1) * CHUNK)
-            total = None
-            for slot in range(2):
-                joined = dot(woutt_ref[slot], taps_ref[:, at]).astype(BF16).astype(F32)
-                middle = (joined * d2_ref[slot, :, at].astype(F32)).astype(BF16)
-                active = dot(wmidt_ref[...], middle).astype(BF16).astype(F32)
-                hidden = (joined + active * d1_ref[slot, :, at].astype(F32)).astype(BF16)
-                inward = dot(wint_ref[slot], hidden)
-                total = inward if total is None else total + inward
-            outward_ref[:, at] = total
-        return summed_taps(outward_ref, -1, True)
+            joined = dot(woutt_ref[slot], taps_ref[:, at]).astype(BF16)
+            held[step, slot] = (joined, joined * d2_ref[slot, :, at])
+
+        def stage_mid(step, slot):
+            at = slice(step * CHUNK, (step + 1) * CHUNK)
+            joined, middle = held[step, slot]
+            active = dot(wmidt_ref[...], middle).astype(BF16)
+            held[step, slot] = joined + active * d1_ref[slot, :, at]
+
+        def stage_in(step, slot):
+            inward = dot(wint_ref[slot], held[step, slot])
+            totals[step] = totals[step] + inward if step in totals else inward
+            if slot == 1:
+                outward_ref[:, step * CHUNK : (step + 1) * CHUNK] = totals[step]
+
+        in_turn(units, (stage_out, stage_mid, stage_in), 2)
+        return summed_taps(outward_ref, -1, False)
 
     def features(tile, slot):
         total = None
@@ -496,7 +574,7 @@
                     grad = jnp.where(row_iota() == slot * 4 + channel, row, grad)
             clean_grad.append(grad)
         pulled = pulled_back([(-now_s / now_a) * grad for grad in clean_grad])
-        gradient = [p + g * (1.0 / now_a) for p, g in zip(pulled, clean_grad)]
+        gradient = [2.0 * p + g * (1.0 / now_a) for p, g in zip(pulled, clean_grad)]
 
         squares = sum(g * g for g in gradient)
         square = jnp.sum(jnp.sum(squares, axis=1, keepdims=True), axis=0, keepdims=True)
@@ -600,21 +678,30 @@
     inner, outer = group_sizes(count)
     most = max(inner, outer)
     vmem = pl.BlockSpec(memory_space=pltpu.VMEM)
-    smem = pl.BlockSpec(memory_space=pltpu.SMEM)
     block = HALF * WIN
     dma = pltpu.SemaphoreType.DMA
     out = pl.pallas_call(
         functools.partial(kernel, count),
         out_shape=jax.ShapeDtypeStruct((32, WIN), F32),
-        in_specs=[vmem, vmem, smem, smem, smem, vmem, vmem, vmem, vmem, vmem],
+        in_specs=[pl.BlockSpec(memory_space=pltpu.HBM)] * 10,
         out_specs=vmem,
         scratch_shapes=[
-            pltpu.VMEM((2, HID, TAPROWS), BF16),
+            pltpu.VMEM((32, WIN), F32),
+            pltpu.VMEM((STEPS * 32, WIN), F32),
+            pltpu.SMEM((2,), jnp.int32),
+            pltpu.SMEM((STEPS,), jnp.int32),
+            pltpu.SMEM((1,), F32),
+            pltpu.VMEM((36, HID), BF16),
+            pltpu.VMEM((HID, HID), BF16),
+            pltpu.VMEM((36, HID), BF16),
+            pltpu.VMEM((STEPS, HID), F32),
+            pltpu.VMEM((4, FEAT), F32),
+            pltpu.VMEM((STEPS, 2, HID, TAPROWS), BF16),
             pltpu.VMEM((2, TAPROWS, HID), BF16),
             pltpu.VMEM((2, TAPROWS, HID), BF16),
             pltpu.VMEM((2, HID, TAPROWS), BF16),
             pltpu.VMEM((HID, HID), BF16),
-            pltpu.VMEM((STEPS, HID, WIN), F32),
+            pltpu.VMEM((HID, HID), BF16),
             pltpu.VMEM((4, FEAT, WIN), F32),
             pltpu.VMEM((TAPROWS, HEIGHT * WIN), BF16),
             pltpu.VMEM((TAPROWS, HEIGHT * WIN), F32),
@@ -645,6 +732,7 @@
             dma((STEPS, 2, 2, most - 1)),
             dma((STEPS, 2, most - 1)),
             dma((STEPS, 2, most - 1)),
+            dma((10,)),
         ],
         compiler_params=pltpu.CompilerParams(collective_id=0, has_side_effects=True),
         name="panorama",

time: 58.4 us -> 51.6 us (0.88)
  Pallas kernels: 56.2 us -> 49.4 us
    pallas_call x1, Pallas kernels: 56.2 us -> 49.4 us  [local(): pl.pallas_call(functools.partial(kernel, count), out_shape=jax.ShapeDtype...]
where the time goes in v3:
time: 51.6 us; the launch traced here: 51.4 us
  Pallas kernels  49.4 us (96%)
  local copies, waits for them, and re-layouts  1.32 us (3%)
  between operations  0.66 us (1%)
    pallas_call x1, Pallas kernels, local(): pl.pallas_call(functools.partial(kernel, count), out_shape=jax.ShapeDtype...  49.4 us
    unnamed x1, local copies, waits for them, and re-layouts  1.32 us

profile of v3, /device:TPU:2, one launch (start us, length us, event | category | flops | bytes accessed | tf_op | source)
XLA Modules:
  0.0 51.4 jit_solution(5585499645262300948)
XLA Ops:
  0.7 49.4 %panorama.1 = f32[32,128]{1,0:T(8,128)} custom-call(f32[32,128]{1,0:T(8,128)} %bitcast.8, f32[64,128]{1,0:T(8,128)} %bitcast.6, s32[2]{0:T(128)} %offsets_hbm.1, s32[2]{0:T(128)} %anchors_hbm.1, f32[1]{0:T(128)S(6)} %copy.12.guidance_hbm, bf16[36,320]{1,0:T(8,128)(2,1)} %bitcast.7, bf16[320,320]{1,0:T(8,128)(2,1)} %w_mid_hbm.1, bf16[36,320]{1,0:T(8,128)(2,1)} %w_out_hbm.1, ...), custom_call_target="tpu_custom_call" | custom-call | tf_op jit(solution)/shard_map/panorama/pallas_call | solution.py:683
  50.1 1.3 %copy.13 = f32[4,8,128]{2,1,0:T(8,128)} copy(f32[4,8,128]{2,1,0:T(8,128)} %bitcast.5) | data formatting | bytes 32768

commit v4 on v3

--- a/solution.py
+++ b/solution.py
@@ -18,7 +18,9 @@
 FEAT = 64
 TAPROWS = 80
 ONES = 72
-CHUNK = 512
+BOTH = (512, 2)
+ALONE = (512, 1)
+BACK = (512, 2)
 MESH = pl.DeviceIdType.MESH
 F32 = jnp.float32
 BF16 = jnp.bfloat16
@@ -108,10 +110,6 @@
             by_shift[0] + sideways(by_shift[-1], -1) + sideways(by_shift[1], 1)
         )
     return tiles
-
-
-def gate_of(value):
-    return 0.5 * jnp.tanh(0.5 * value) + 0.5
 
 
 def silu_of_half(half):
@@ -173,6 +171,8 @@
     d1_ref,
     d2_ref,
     percept_ref,
+    active_ref,
+    slope_ref,
     halo_src,
     halo_dst,
     cover_src,
@@ -238,7 +238,7 @@
     ]
     for load in loads:
         load.start()
-    first_loads, weights = loads[:4], loads[4:]
+    first_loads, later_loads = loads[:3], loads[3:]
 
     def arrive(some):
         for load in some:
@@ -283,25 +283,237 @@
         return [ref[(*index, slice(None), slice(t * WIN, (t + 1) * WIN))] for t in range(size)]
 
     own = packed(latent_ref, 0)
-    noise = [packed(noise_ref, 32 * number) for number in range(STEPS)]
     put(halo_src, (0,), own)
-    put(halo_src, (1,), noise[0])
     cover_own = sum(flag(lanes >= start) for start in starts)
     cover_next = sum(flag(lanes < start) for start in starts)
     cover_src[0] = cover_own
     cover_src[1] = cover_next
 
-    shares = []
-    for number in range(STEPS):
-        mine = [flag(anchors_ref[number] == 2 * me + slot) for slot in range(2)]
-        shares.append(
-            mine[0] * offsets_ref[0].astype(F32) + mine[1] * offsets_ref[1].astype(F32)
-        )
+    odd = slots_of[0].astype(F32)
     is_first = flag(owners[0] == me)
     is_second = flag(owners[0] == left)
-    put(casts_a, (0, 0), [tile * is_first for tile in own])
-    casts_a[0, 0, :, HALF * WIN :] = jnp.where(row_iota() < 4, shares[0], shares[1])
-    put(casts_b, (0, 0), [tile * is_second for tile in own])
+    whole = is_first * (1.0 - odd) + is_second * odd
+    upper = is_first * odd
+    lower = is_second * (1.0 - odd)
+    turned = [pltpu.roll(tile, STRIDE, 1) for tile in own]
+    halves = []
+    for tile in (0, 2):
+        low = jnp.where(lanes < STRIDE, own[tile], turned[tile + 1])
+        high = jnp.where(lanes < STRIDE, turned[tile], own[tile + 1])
+        halves.append(lower * low + upper * high)
+    near = anchors_ref[1] + row_iota() - 3
+    near = jnp.where(near < 0, near + 2 * count, near)
+    near = jnp.where(near >= 2 * count, near - 2 * count, near)
+    near = jnp.where(row_iota() == 0, anchors_ref[0], near)
+    share = sum(
+        jnp.where(near == 2 * me + slot, offsets_ref[slot].astype(F32), 0.0) for slot in range(2)
+    )
+    put(casts_a, (0, 0), [own[0] * whole, own[1] * whole, halves[0], share])
+    put(casts_b, (0, 0), [own[2] * whole, own[3] * whole, halves[1]])
+
+    def denoised(tiles, number, slots, keep):
+        store_taps(taps_ref, tiles, 1)
+        chunk, apart = BOTH if keep else ALONE
+        units = [(step, slot) for step in range(HEIGHT * WIN // chunk) for slot in slots]
+        held, totals = {}, {}
+
+        def stage_in(step, slot):
+            at = slice(step * chunk, (step + 1) * chunk)
+            hidden = dot(win_ref[number, slot], taps_ref[:, at])
+            half = hidden.astype(BF16)
+            active, slope = silu_of_half(half)
+            if keep:
+                d1_ref[slot, :, at] = slope
+            held[step, slot] = (hidden, active)
+
+        def stage_mid(step, slot):
+            at = slice(step * chunk, (step + 1) * chunk)
+            hidden, active = held[step, slot]
+            middle = dot(wmid_ref[...], active)
+            active, slope = silu_of_half(middle.astype(BF16))
+            if keep:
+                d2_ref[slot, :, at] = slope
+            held[step, slot] = (hidden + hidden + active.astype(F32)).astype(BF16)
+
+        def stage_out(step, slot):
+            outward = dot(wout_ref[slot], held[step, slot])
+            totals[step] = totals[step] + outward if step in totals else outward
+            if slot == slots[-1]:
+                outward_ref[:, step * chunk : (step + 1) * chunk] = totals[step]
+
+        in_turn(units, (stage_in, stage_mid, stage_out), apart)
+        return summed_taps(outward_ref, 1, False)
+
+    def pulled_back(tiles):
+        store_taps(taps_ref, tiles, -1)
+        chunk, apart = BACK
+        units = [(step, slot) for step in range(HEIGHT * WIN // chunk) for slot in range(2)]
+        held, totals = {}, {}
+
+        def stage_out(step, slot):
+            at = slice(step * chunk, (step + 1) * chunk)
+            joined = dot(woutt_ref[slot], taps_ref[:, at]).astype(BF16)
+            held[step, slot] = (joined, joined * d2_ref[slot, :, at])
+
+        def stage_mid(step, slot):
+            at = slice(step * chunk, (step + 1) * chunk)
+            joined, middle = held[step, slot]
+            active = dot(wmidt_ref[...], middle).astype(BF16)
+            held[step, slot] = joined + active * d1_ref[slot, :, at]
+
+        def stage_in(step, slot):
+            inward = dot(wint_ref[slot], held[step, slot])
+            totals[step] = totals[step] + inward if step in totals else inward
+            if slot == 1:
+                outward_ref[:, step * chunk : (step + 1) * chunk] = totals[step]
+
+        in_turn(units, (stage_out, stage_mid, stage_in), apart)
+        return summed_taps(outward_ref, -1, False)
+
+    def features(tile, slot):
+        total = None
+        for channel in range(4):
+            row = tile[slot * 4 + channel : slot * 4 + channel + 1, :]
+            term = feat_ref[channel] * row
+            total = term if total is None else total + term
+        return total
+
+    def cut(first, second, start):
+        back = lax.rem(WIN - start, WIN)
+        return [
+            jnp.where(
+                lanes < WIN - start,
+                pltpu.roll(first[tile], back, 1),
+                pltpu.roll(second[tile], back, 1),
+            )
+            for tile in range(HALF)
+        ]
+
+    def windows_of(first, second):
+        both = [cut(first, second, start) for start in starts]
+        tiles = [low_high(both[0][tile], swapped(both[1][tile])) for tile in range(HALF)]
+        tiles += [low_high(swapped(both[0][tile]), both[1][tile]) for tile in range(HALF)]
+        return tiles
+
+    def pieces_of(tiles):
+        lows, highs = tiles[:HALF], tiles[HALF:]
+        return (
+            [low_high(low, swapped(high)) for low, high in zip(lows, highs)],
+            [low_high(swapped(low), high) for low, high in zip(lows, highs)],
+        )
+
+    def placed(pieces):
+        turned = [
+            [pltpu.roll(tile, start, 1) for tile in piece]
+            for piece, start in zip(pieces, starts)
+        ]
+        pairs = list(zip(*turned))
+        own_sum = [
+            sum(jnp.where(lanes >= start, t, 0.0) for t, start in zip(pair, starts))
+            for pair in pairs
+        ]
+        next_sum = [
+            sum(jnp.where(lanes < start, t, 0.0) for t, start in zip(pair, starts))
+            for pair in pairs
+        ]
+        return own_sum, next_sum
+
+    def far_first(size):
+        return sorted(range(1, size), key=lambda by: -min(by, size - by))
+
+    def exchange(along_inner, source, target, send, recv, size=None):
+        started = []
+        for by in far_first(inner if along_inner else outer):
+            peer = inner_peer(by) if along_inner else outer_peer(by)
+            landing = target.at[by - 1]
+            if size is not None:
+                landing = landing.at[:, :size]
+            copy = remote(source, landing, send.at[by - 1], recv.at[by - 1], peer)
+            copy.start()
+            started.append((by, copy))
+        return started
+
+    def finish(started, total, target, size=None):
+        for by, copy in started:
+            copy.wait_recv()
+            part = target[by - 1]
+            total = total + (part if size is None else part[:, :size])
+        return total
+
+    sent = []
+
+    def width_of(number, half):
+        return (HALF - 1 if number == 0 and half == 1 else HALF) * WIN
+
+    def cast_start(number):
+        return [
+            exchange(
+                half == 0,
+                (casts_a, casts_b)[half].at[number, 0, :, : width_of(number, half)],
+                (firsts_a, firsts_b)[half].at[number],
+                cast_send.at[number, 0, half],
+                cast_recv.at[number, 0, half],
+                width_of(number, half),
+            )
+            for half in range(2)
+        ]
+
+    def cast_middle(number, started):
+        out = []
+        for half in range(2):
+            size = width_of(number, half)
+            source = (casts_a, casts_b)[half]
+            source[number, 1, :, :size] = finish(
+                started[half],
+                source[number, 0, :, :size],
+                (firsts_a, firsts_b)[half].at[number],
+                size,
+            )
+            out.append(
+                exchange(
+                    half == 1,
+                    source.at[number, 1, :, :size],
+                    (seconds_a, seconds_b)[half].at[number],
+                    cast_send.at[number, 1, half],
+                    cast_recv.at[number, 1, half],
+                    size,
+                )
+            )
+            sent.extend(started[half])
+        return out
+
+    def cast_end(number, started):
+        out = []
+        for half in range(2):
+            size = width_of(number, half)
+            total = finish(
+                started[half],
+                (casts_a, casts_b)[half][number, 1, :, :size],
+                (seconds_a, seconds_b)[half].at[number],
+                size,
+            )
+            out.append([total[:, t * WIN : (t + 1) * WIN] for t in range(size // WIN)])
+            sent.extend(started[half])
+        return out
+
+    pl.semaphore_wait(barrier, len(peers))
+
+    started = cast_start(0)
+    copies = [
+        remote(halo_src.at[0], halo_dst.at[0], edge_send.at[0], edge_recv.at[0], left),
+        remote(cover_src.at[0], cover_dst.at[0], edge_send.at[2], edge_recv.at[2], left),
+        remote(cover_src.at[1], cover_dst.at[1], edge_send.at[3], edge_recv.at[3], right),
+    ]
+    for copy in copies:
+        copy.start()
+    arrive(later_loads)
+    noise = [packed(noise_ref, 32 * number) for number in range(STEPS)]
+    put(halo_src, (1,), noise[0])
+    copies.append(
+        remote(halo_src.at[1], halo_dst.at[1], edge_send.at[1], edge_recv.at[1], left)
+    )
+    copies[-1].start()
+    sent += [(0, copy) for copy in copies]
 
     def one_hot(slot):
         wide = lax.broadcasted_iota(jnp.int32, (TAPROWS, 36), 0)
@@ -314,7 +526,6 @@
         == lax.broadcasted_iota(jnp.int32, (HID, HID), 1)
     )
     eye_b = eye.astype(BF16)
-    arrive(weights)
     w_in = w_in_ref[...]
     w_out = w_out_ref[...]
     tap_rows = lax.broadcasted_iota(jnp.int32, (TAPROWS, HID), 0)
@@ -339,192 +550,15 @@
         column = jnp.sum(
             eye[:FEAT, :FEAT] * w_feat_ref[channel : channel + 1, :], axis=1, keepdims=True
         )
-        feat_ref[channel] = jnp.broadcast_to(column, (FEAT, WIN))
-
-    def denoised(tiles, number, slots, keep):
-        store_taps(taps_ref, tiles, 1)
-        units = [(step, slot) for step in range(HEIGHT * WIN // CHUNK) for slot in slots]
-        held, totals = {}, {}
-
-        def stage_in(step, slot):
-            at = slice(step * CHUNK, (step + 1) * CHUNK)
-            hidden = dot(win_ref[number, slot], taps_ref[:, at])
-            half = hidden.astype(BF16)
-            active, slope = silu_of_half(half)
-            if keep:
-                d1_ref[slot, :, at] = slope
-            held[step, slot] = (hidden, active)
-
-        def stage_mid(step, slot):
-            at = slice(step * CHUNK, (step + 1) * CHUNK)
-            hidden, active = held[step, slot]
-            middle = dot(wmid_ref[...], active)
-            active, slope = silu_of_half(middle.astype(BF16))
-            if keep:
-                d2_ref[slot, :, at] = slope
-            held[step, slot] = (hidden + hidden + active.astype(F32)).astype(BF16)
-
-        def stage_out(step, slot):
-            outward = dot(wout_ref[slot], held[step, slot])
-            totals[step] = totals[step] + outward if step in totals else outward
-            if slot == slots[-1]:
-                outward_ref[:, step * CHUNK : (step + 1) * CHUNK] = totals[step]
-
-        in_turn(units, (stage_in, stage_mid, stage_out), 2)
-        return summed_taps(outward_ref, 1, False)
-
-    def pulled_back(tiles):
-        store_taps(taps_ref, tiles, -1)
-        units = [(step, slot) for step in range(HEIGHT * WIN // CHUNK) for slot in range(2)]
-        held, totals = {}, {}
-
-        def stage_out(step, slot):
-            at = slice(step * CHUNK, (step + 1) * CHUNK)
-            joined = dot(woutt_ref[slot], taps_ref[:, at]).astype(BF16)
-            held[step, slot] = (joined, joined * d2_ref[slot, :, at])
-
-        def stage_mid(step, slot):
-            at = slice(step * CHUNK, (step + 1) * CHUNK)
-            joined, middle = held[step, slot]
-            active = dot(wmidt_ref[...], middle).astype(BF16)
-            held[step, slot] = joined + active * d1_ref[slot, :, at]
-
-        def stage_in(step, slot):
-            inward = dot(wint_ref[slot], held[step, slot])
-            totals[step] = totals[step] + inward if step in totals else inward
-            if slot == 1:
-                outward_ref[:, step * CHUNK : (step + 1) * CHUNK] = totals[step]
-
-        in_turn(units, (stage_out, stage_mid, stage_in), 2)
-        return summed_taps(outward_ref, -1, False)
-
-    def features(tile, slot):
-        total = None
-        for channel in range(4):
-            row = tile[slot * 4 + channel : slot * 4 + channel + 1, :]
-            term = feat_ref[channel] * row
-            total = term if total is None else total + term
-        return total
-
-    def cut(first, second, start):
-        back = lax.rem(WIN - start, WIN)
-        return [
-            jnp.where(
-                lanes < WIN - start,
-                pltpu.roll(first[tile], back, 1),
-                pltpu.roll(second[tile], back, 1),
-            )
-            for tile in range(HALF)
-        ]
-
-    def windows_of(first, second):
-        both = [cut(first, second, start) for start in starts]
-        tiles = [low_high(both[0][tile], swapped(both[1][tile])) for tile in range(HALF)]
-        tiles += [low_high(swapped(both[0][tile]), both[1][tile]) for tile in range(HALF)]
-        return tiles
-
-    def pieces_of(tiles):
-        lows, highs = tiles[:HALF], tiles[HALF:]
-        return (
-            [low_high(low, swapped(high)) for low, high in zip(lows, highs)],
-            [low_high(swapped(low), high) for low, high in zip(lows, highs)],
-        )
-
-    def placed(pieces):
-        turned = [
-            [pltpu.roll(tile, start, 1) for tile in piece]
-            for piece, start in zip(pieces, starts)
-        ]
-        pairs = list(zip(*turned))
-        own_sum = [
-            sum(jnp.where(lanes >= start, t, 0.0) for t, start in zip(pair, starts))
-            for pair in pairs
-        ]
-        next_sum = [
-            sum(jnp.where(lanes < start, t, 0.0) for t, start in zip(pair, starts))
-            for pair in pairs
-        ]
-        return own_sum, next_sum
-
-    def far_first(size):
-        return sorted(range(1, size), key=lambda by: -min(by, size - by))
-
-    def exchange(along_inner, source, target, send, recv):
-        started = []
-        for by in far_first(inner if along_inner else outer):
-            peer = inner_peer(by) if along_inner else outer_peer(by)
-            copy = remote(source, target.at[by - 1], send.at[by - 1], recv.at[by - 1], peer)
-            copy.start()
-            started.append((by, copy))
-        return started
-
-    def finish(started, source, target):
-        total = source[...]
-        for by, copy in started:
-            copy.wait_recv()
-            total = total + target[by - 1]
-        return total
-
-    sent = []
-
-    def cast_start(number):
-        return [
-            exchange(
-                half == 0,
-                (casts_a, casts_b)[half].at[number, 0],
-                (firsts_a, firsts_b)[half].at[number],
-                cast_send.at[number, 0, half],
-                cast_recv.at[number, 0, half],
-            )
-            for half in range(2)
-        ]
-
-    def cast_middle(number, started):
-        out = []
-        for half in range(2):
-            source = (casts_a, casts_b)[half].at[number]
-            source[1] = finish(started[half], source.at[0], (firsts_a, firsts_b)[half].at[number])
-            out.append(
-                exchange(
-                    half == 1,
-                    source.at[1],
-                    (seconds_a, seconds_b)[half].at[number],
-                    cast_send.at[number, 1, half],
-                    cast_recv.at[number, 1, half],
-                )
-            )
-            sent.extend(started[half])
-        return out
-
-    def cast_end(number, started):
-        out = []
-        for half in range(2):
-            source = (casts_a, casts_b)[half].at[number, 1]
-            total = finish(started[half], source, (seconds_a, seconds_b)[half].at[number])
-            out.append([total[:, t * WIN : (t + 1) * WIN] for t in range(total.shape[1] // WIN)])
-            sent.extend(started[half])
-        return out
-
-    pl.semaphore_wait(barrier, len(peers))
-
-    started = cast_start(0)
-    copies = [
-        remote(halo_src.at[0], halo_dst.at[0], edge_send.at[0], edge_recv.at[0], left),
-        remote(cover_src.at[0], cover_dst.at[0], edge_send.at[2], edge_recv.at[2], left),
-        remote(cover_src.at[1], cover_dst.at[1], edge_send.at[3], edge_recv.at[3], right),
-        remote(halo_src.at[1], halo_dst.at[1], edge_send.at[1], edge_recv.at[1], left),
-    ]
-    for copy in copies:
-        copy.start()
-        sent.append((0, copy))
+        feat_ref[channel] = jnp.broadcast_to(0.5 * column, (FEAT, WIN))
+
     started = cast_middle(0, started)
     copies[0].wait_recv()
-    following = got(halo_dst, 0)
+    tiles = windows_of(own, got(halo_dst, 0))
 
     for number in range(STEPS):
         now_a, now_s, next_a, direction, spread = plan(number)
         last = number == STEPS - 1
-        tiles = windows_of(own, following)
         predicted = denoised(tiles, number, (0, 1), True)
         cleaned = [(x - now_s * p) * (1.0 / now_a) for x, p in zip(tiles, predicted)]
         base = pieces_of(
@@ -539,42 +573,58 @@
             per_next = 1.0 / (cover_next + cover_dst[0])
             noise_next = got(halo_dst, 1)
 
+        for slot in range(2):
+            for h in range(HEIGHT):
+                active, slope = silu_of_half(features(cleaned[h], slot))
+                active_ref[slot, h] = active
+                slope_ref[slot, h] = slope
+
         totals = cast_end(number, started)
         if number == 0:
+            shared = totals[0][3]
             anchor_starts = [
                 slots_of[step] * STRIDE
-                + jnp.max(totals[0][HALF][4 * step : 4 * step + 1, :]).astype(jnp.int32)
+                + jnp.max(shared[(0, 3)[step] : (0, 3)[step] + 1, :]).astype(jnp.int32)
                 for step in range(STEPS)
             ]
-            picked = cut(totals[0][:HALF], totals[1], anchor_starts[0])
+            whole = totals[0][:2] + totals[1][:2]
+            halves = [totals[0][2], totals[1][2]]
+            turned = [pltpu.roll(tile, STRIDE, 1) for tile in halves]
+            low = [halves[0], turned[0], halves[1], turned[1]]
+            high = [turned[0], halves[0], turned[1], halves[1]]
+            picked = cut(
+                [w * (1.0 - odd) + h * odd for w, h in zip(whole, high)],
+                [w * odd + l * (1.0 - odd) for w, l in zip(whole, low)],
+                anchor_starts[0],
+            )
+            places = lanes.astype(F32)
+            counted = jnp.zeros((ROWS, WIN), F32)
+            for gap in range(-2, 3):
+                ahead = shared[gap + 3 : gap + 4, :] - shared[3:4, :] + float(gap * STRIDE)
+                counted = counted + flag((places >= ahead) & (places < ahead + WIN))
+            per_anchor = 1.0 / counted
         else:
-            factor = 1.0 / totals[0][HALF]
             picked = [
-                (totals[t // 2][t % 2] - scale * totals[t // 2][2 + t % 2]) * factor
+                (totals[t // 2][t % 2] - scale * totals[t // 2][2 + t % 2]) * per_anchor
                 for t in range(HALF)
             ]
         anchor_tiles = picked + [swapped(tile) for tile in picked]
         anchor_predicted = denoised(anchor_tiles, number, (0,), False)
         for h in range(HEIGHT):
             clean = (anchor_tiles[h] - now_s * anchor_predicted[h]) * (1.0 / now_a)
-            value = features(clean, 0)
-            percept_ref[h] = value * gate_of(value)
+            percept_ref[h] = silu_of_half(features(clean, 0))[0]
 
         clean_grad = []
         for h in range(HEIGHT):
             grad = jnp.zeros((ROWS, WIN), F32)
             for slot in range(2):
-                value = features(cleaned[h], slot)
-                gate = gate_of(value)
-                active = value * gate
-                slope = gate + active * (1.0 - gate)
-                pull = (active - percept_ref[h]) * slope * (1.0 / FEAT)
+                pull = (active_ref[slot, h] - percept_ref[h]) * slope_ref[slot, h]
                 for channel in range(4):
                     row = jnp.sum(feat_ref[channel] * pull, axis=0, keepdims=True)
                     grad = jnp.where(row_iota() == slot * 4 + channel, row, grad)
             clean_grad.append(grad)
-        pulled = pulled_back([(-now_s / now_a) * grad for grad in clean_grad])
-        gradient = [2.0 * p + g * (1.0 / now_a) for p, g in zip(pulled, clean_grad)]
+        pulled = pulled_back([(-now_s / now_a / FEAT) * grad for grad in clean_grad])
+        gradient = [2.0 * p + g * (1.0 / now_a / FEAT) for p, g in zip(pulled, clean_grad)]
 
         squares = sum(g * g for g in gradient)
         square = jnp.sum(jnp.sum(squares, axis=1, keepdims=True), axis=0, keepdims=True)
@@ -607,8 +657,7 @@
             grad_part = [
                 a + b for a, b in zip(*[framed(piece, gap) for piece, gap in zip(grads, gaps)])
             ]
-            cover = sum(flag((lanes >= gap) & (lanes < gap + WIN)) for gap in gaps)
-            put(casts_a, (1, 0), base_part[:2] + grad_part[:2] + [cover])
+            put(casts_a, (1, 0), base_part[:2] + grad_part[:2])
             put(casts_b, (1, 0), base_part[2:] + grad_part[2:])
             started = cast_start(1)
 
@@ -633,7 +682,7 @@
             to_left.start()
             sent.append((0, to_left))
 
-        square_mid[number] = finish(first, square_src.at[number], square_first.at[number])
+        square_mid[number] = finish(first, square_src[number], square_first.at[number])
         second = exchange(
             False,
             square_mid.at[number],
@@ -651,25 +700,27 @@
             to_left.wait_recv()
             base_far = got(sums_left_dst, 0)
             grad_far = got(sums_left_dst, 1)
-        total = finish(second, square_mid.at[number], square_second.at[number])
+        own_base = [
+            (b + c) * per_own + spread * n for b, c, n in zip(base_own, base_in, noise[number])
+        ]
+        own_grad = [(g + c) * per_own for g, c in zip(grad_own, grad_in)]
+        if last:
+            parts = (own_base, own_grad)
+        else:
+            next_base = [
+                (b + c) * per_next + spread * n for b, c, n in zip(base_next, base_far, noise_next)
+            ]
+            next_grad = [(g + c) * per_next for g, c in zip(grad_next, grad_far)]
+            parts = (windows_of(own_base, next_base), windows_of(own_grad, next_grad))
+        total = finish(second, square_mid[number], square_second.at[number])
         entries = 2 * count * 4 * HEIGHT * WIN
         scale = guidance_ref[0] * lax.rsqrt(total * (1.0 / entries) + STABILITY)
         scale = (next_a / now_a) * scale
-        own = [
-            (base_own[t] + base_in[t] - scale * (grad_own[t] + grad_in[t])) * per_own
-            + spread * noise[number][t]
-            for t in range(HALF)
-        ]
-        if not last:
-            following = [
-                (base_next[t] + base_far[t] - scale * (grad_next[t] + grad_far[t])) * per_next
-                + spread * noise_next[t]
-                for t in range(HALF)
-            ]
+        tiles = [b - scale * g for b, g in zip(*parts)]
 
     for tile in range(HALF):
-        out_ref[pl.ds(tile, 4, stride=8), :] = own[tile][:4]
-        out_ref[pl.ds(tile + HALF, 4, stride=8), :] = own[tile][4:]
+        out_ref[pl.ds(tile, 4, stride=8), :] = tiles[tile][:4]
+        out_ref[pl.ds(tile + HALF, 4, stride=8), :] = tiles[tile][4:]
     for _, copy in sent:
         copy.wait_send()
 
@@ -708,6 +759,8 @@
             pltpu.VMEM((2, HID, HEIGHT * WIN), BF16),
             pltpu.VMEM((2, HID, HEIGHT * WIN), BF16),
             pltpu.VMEM((HEIGHT, FEAT, WIN), F32),
+            pltpu.VMEM((2, HEIGHT, FEAT, WIN), F32),
+            pltpu.VMEM((2, HEIGHT, FEAT, WIN), F32),
             pltpu.VMEM((2, ROWS, block), F32),
             pltpu.VMEM((2, ROWS, block), F32),
             pltpu.VMEM((2, ROWS, WIN), F32),
@@ -716,11 +769,11 @@
             pltpu.VMEM((2, ROWS, block), F32),
             pltpu.VMEM((STEPS, 2, ROWS, block), F32),
             pltpu.VMEM((STEPS, 2, ROWS, block), F32),
-            pltpu.VMEM((STEPS, 2, ROWS, block + WIN), F32),
             pltpu.VMEM((STEPS, 2, ROWS, block), F32),
-            pltpu.VMEM((STEPS, inner - 1, ROWS, block + WIN), F32),
+            pltpu.VMEM((STEPS, 2, ROWS, block), F32),
+            pltpu.VMEM((STEPS, inner - 1, ROWS, block), F32),
             pltpu.VMEM((STEPS, outer - 1, ROWS, block), F32),
-            pltpu.VMEM((STEPS, outer - 1, ROWS, block + WIN), F32),
+            pltpu.VMEM((STEPS, outer - 1, ROWS, block), F32),
             pltpu.VMEM((STEPS, inner - 1, ROWS, block), F32),
             pltpu.VMEM((STEPS, 1, WIN), F32),
             pltpu.VMEM((STEPS, 1, WIN), F32),

time: 51.6 us -> 50.9 us (0.986)
  Pallas kernels: 49.4 us -> 48.8 us
    pallas_call x1, Pallas kernels: 49.4 us -> 48.8 us  [local(): pl.pallas_call(functools.partial(kernel, count), out_shape=jax.ShapeDtype...]
where the time goes in v4:
time: 50.9 us; the launch traced here: 50.8 us
  Pallas kernels  48.8 us (96%)
  local copies, waits for them, and re-layouts  1.32 us (3%)
  between operations  0.66 us (1%)
    pallas_call x1, Pallas kernels, local(): pl.pallas_call(functools.partial(kernel, count), out_shape=jax.ShapeDtype...  48.8 us
    unnamed x1, local copies, waits for them, and re-layouts  1.32 us

profile of v4, /device:TPU:2, one launch (start us, length us, event | category | flops | bytes accessed | tf_op | source)
XLA Modules:
  0.0 50.8 jit_solution(13275267017663943300)
XLA Ops:
  0.7 48.8 %panorama.1 = f32[32,128]{1,0:T(8,128)} custom-call(f32[32,128]{1,0:T(8,128)} %bitcast.8, f32[64,128]{1,0:T(8,128)} %bitcast.6, s32[2]{0:T(128)} %offsets_hbm.1, s32[2]{0:T(128)} %anchors_hbm.1, f32[1]{0:T(128)S(6)} %copy.12.guidance_hbm, bf16[36,320]{1,0:T(8,128)(2,1)} %bitcast.7, bf16[320,320]{1,0:T(8,128)(2,1)} %w_mid_hbm.1, bf16[36,320]{1,0:T(8,128)(2,1)} %w_out_hbm.1, ...), custom_call_target="tpu_custom_call" | custom-call | tf_op jit(solution)/shard_map/panorama/pallas_call | solution.py:734
  49.4 1.3 %copy.13 = f32[4,8,128]{2,1,0:T(8,128)} copy(f32[4,8,128]{2,1,0:T(8,128)} %bitcast.5) | data formatting | bytes 32768

commit v5 on v4

--- a/solution.py
+++ b/solution.py
@@ -188,9 +188,7 @@
     seconds_a,
     seconds_b,
     square_src,
-    square_mid,
-    square_first,
-    square_second,
+    square_dst,
     edge_send,
     edge_recv,
     cast_send,
@@ -417,6 +415,16 @@
             for pair in pairs
         ]
         return own_sum, next_sum
+
+    everyone = [
+        (by_inner, by_outer)
+        for by_inner in range(inner)
+        for by_outer in range(outer)
+        if by_inner + by_outer > 0
+    ]
+    everyone.sort(
+        key=lambda by: -min(by[0], inner - by[0]) - min(by[1] % 4, 4 - by[1] % 4) - by[1] // 4
+    )
 
     def far_first(size):
         return sorted(range(1, size), key=lambda by: -min(by, size - by))
@@ -629,13 +637,19 @@
         squares = sum(g * g for g in gradient)
         square = jnp.sum(jnp.sum(squares, axis=1, keepdims=True), axis=0, keepdims=True)
         square_src[number] = jnp.broadcast_to(square, (1, WIN))
-        first = exchange(
-            True,
-            square_src.at[number],
-            square_first.at[number],
-            square_send.at[number, 0],
-            square_recv.at[number, 0],
-        )
+        spread_square = []
+        for by_inner, by_outer in everyone:
+            index = by_outer * inner + by_inner - 1
+            copy = remote(
+                square_src.at[number],
+                square_dst.at[number, index],
+                square_send.at[number, index],
+                square_recv.at[number, index],
+                lax.rem(my_outer + by_outer, outer) * inner + lax.rem(my_inner + by_inner, inner),
+            )
+            copy.start()
+            spread_square.append((index, copy))
+        sent += spread_square
 
         grads = pieces_of(gradient)
         if not last:
@@ -682,15 +696,6 @@
             to_left.start()
             sent.append((0, to_left))
 
-        square_mid[number] = finish(first, square_src[number], square_first.at[number])
-        second = exchange(
-            False,
-            square_mid.at[number],
-            square_second.at[number],
-            square_send.at[number, 1],
-            square_recv.at[number, 1],
-        )
-        sent += first + second
         if not last:
             started = cast_middle(1, started)
         to_right.wait_recv()
@@ -712,9 +717,11 @@
             ]
             next_grad = [(g + c) * per_next for g, c in zip(grad_next, grad_far)]
             parts = (windows_of(own_base, next_base), windows_of(own_grad, next_grad))
-        total = finish(second, square_mid[number], square_second.at[number])
+        for _, copy in spread_square:
+            copy.wait_recv()
+        total = square_src[number] + jnp.sum(square_dst[number], axis=0)
         entries = 2 * count * 4 * HEIGHT * WIN
-        scale = guidance_ref[0] * lax.rsqrt(total * (1.0 / entries) + STABILITY)
+        scale = guidance_ref[0, 0] * lax.rsqrt(total * (1.0 / entries) + STABILITY)
         scale = (next_a / now_a) * scale
         tiles = [b - scale * g for b, g in zip(*parts)]
 
@@ -741,7 +748,7 @@
             pltpu.VMEM((STEPS * 32, WIN), F32),
             pltpu.SMEM((2,), jnp.int32),
             pltpu.SMEM((STEPS,), jnp.int32),
-            pltpu.SMEM((1,), F32),
+            pltpu.SMEM((1, 1), F32),
             pltpu.VMEM((36, HID), BF16),
             pltpu.VMEM((HID, HID), BF16),
             pltpu.VMEM((36, HID), BF16),
@@ -776,15 +783,13 @@
             pltpu.VMEM((STEPS, outer - 1, ROWS, block), F32),
             pltpu.VMEM((STEPS, inner - 1, ROWS, block), F32),
             pltpu.VMEM((STEPS, 1, WIN), F32),
-            pltpu.VMEM((STEPS, 1, WIN), F32),
-            pltpu.VMEM((STEPS, inner - 1, 1, WIN), F32),
-            pltpu.VMEM((STEPS, outer - 1, 1, WIN), F32),
+            pltpu.VMEM((STEPS, count - 1, 1, WIN), F32),
             dma((7,)),
             dma((7,)),
             dma((STEPS, 2, 2, most - 1)),
             dma((STEPS, 2, 2, most - 1)),
-            dma((STEPS, 2, most - 1)),
-            dma((STEPS, 2, most - 1)),
+            dma((STEPS, count - 1)),
+            dma((STEPS, count - 1)),
             dma((10,)),
         ],
         compiler_params=pltpu.CompilerParams(collective_id=0, has_side_effects=True),
@@ -794,7 +799,7 @@
         noise.reshape(STEPS * 32, WIN),
         offsets,
         anchors,
-        guidance,
+        guidance.reshape(1, 1),
         w_in.T,
         w_mid,
         w_out,

time: 50.9 us -> 50.3 us (0.988)
  Pallas kernels: 48.8 us -> 48.2 us
    pallas_call x1, Pallas kernels: 48.8 us -> 48.2 us  [local(): pl.pallas_call(functools.partial(kernel, count), out_shape=jax.ShapeDtype...]
where the time goes in v5:
time: 50.3 us; the launch traced here: 50.1 us
  Pallas kernels  48.2 us (96%)
  local copies, waits for them, and re-layouts  1.32 us (3%)
  between operations  0.66 us (1%)
    pallas_call x1, Pallas kernels, local(): pl.pallas_call(functools.partial(kernel, count), out_shape=jax.ShapeDtype...  48.2 us
    unnamed x1, local copies, waits for them, and re-layouts  1.32 us

profile of v5, /device:TPU:2, one launch (start us, length us, event | category | flops | bytes accessed | tf_op | source)
XLA Modules:
  0.0 50.1 jit_solution(12792849082480396062)
XLA Ops:
  0.7 48.2 %panorama.1 = f32[32,128]{1,0:T(8,128)} custom-call(f32[32,128]{1,0:T(8,128)} %bitcast.10, f32[64,128]{1,0:T(8,128)} %bitcast.8, s32[2]{0:T(128)} %offsets_hbm.1, s32[2]{0:T(128)} %anchors_hbm.1, f32[1,1]{1,0:T(1,128)} %bitcast.6.guidance_hbm, bf16[36,320]{1,0:T(8,128)(2,1)} %bitcast.9, bf16[320,320]{1,0:T(8,128)(2,1)} %w_mid_hbm.1, ...), custom_call_target="tpu_custom_call" | custom-call | tf_op jit(solution)/shard_map/panorama/pallas_call | solution.py:741
  48.8 1.3 %copy.13 = f32[4,8,128]{2,1,0:T(8,128)} copy(f32[4,8,128]{2,1,0:T(8,128)} %bitcast.7) | data formatting | bytes 32768

commit v6 on v5

--- a/solution.py
+++ b/solution.py
@@ -429,23 +429,29 @@
     def far_first(size):
         return sorted(range(1, size), key=lambda by: -min(by, size - by))
 
-    def exchange(along_inner, source, target, send, recv, size=None):
-        started = []
+    class Batch:
+        def __init__(self, copies, landing, send, recv):
+            self.landing, self.send, self.recv = landing, send, recv
+            for copy in copies:
+                copy.start()
+
+        def wait_recv(self):
+            pltpu.make_async_copy(self.landing, self.landing, self.recv).wait()
+
+        def wait_send(self):
+            pltpu.make_async_copy(self.landing, self.landing, self.send).wait()
+
+    def exchange(along_inner, source, target, send, recv):
+        copies = []
         for by in far_first(inner if along_inner else outer):
             peer = inner_peer(by) if along_inner else outer_peer(by)
-            landing = target.at[by - 1]
-            if size is not None:
-                landing = landing.at[:, :size]
-            copy = remote(source, landing, send.at[by - 1], recv.at[by - 1], peer)
-            copy.start()
-            started.append((by, copy))
-        return started
-
-    def finish(started, total, target, size=None):
-        for by, copy in started:
-            copy.wait_recv()
-            part = target[by - 1]
-            total = total + (part if size is None else part[:, :size])
+            copies.append(remote(source, target.at[by - 1], send, recv, peer))
+        return Batch(copies, target, send, recv)
+
+    def finish(batch, total):
+        batch.wait_recv()
+        for index in range(batch.landing.shape[0]):
+            total = total + batch.landing[index]
         return total
 
     sent = []
@@ -458,10 +464,9 @@
             exchange(
                 half == 0,
                 (casts_a, casts_b)[half].at[number, 0, :, : width_of(number, half)],
-                (firsts_a, firsts_b)[half].at[number],
+                (firsts_a, firsts_b)[half].at[number, :, :, : width_of(number, half)],
                 cast_send.at[number, 0, half],
                 cast_recv.at[number, 0, half],
-                width_of(number, half),
             )
             for half in range(2)
         ]
@@ -471,37 +476,26 @@
         for half in range(2):
             size = width_of(number, half)
             source = (casts_a, casts_b)[half]
-            source[number, 1, :, :size] = finish(
-                started[half],
-                source[number, 0, :, :size],
-                (firsts_a, firsts_b)[half].at[number],
-                size,
-            )
+            source[number, 1, :, :size] = finish(started[half], source[number, 0, :, :size])
             out.append(
                 exchange(
                     half == 1,
                     source.at[number, 1, :, :size],
-                    (seconds_a, seconds_b)[half].at[number],
+                    (seconds_a, seconds_b)[half].at[number, :, :, :size],
                     cast_send.at[number, 1, half],
                     cast_recv.at[number, 1, half],
-                    size,
                 )
             )
-            sent.extend(started[half])
+            sent.append(started[half])
         return out
 
     def cast_end(number, started):
         out = []
         for half in range(2):
             size = width_of(number, half)
-            total = finish(
-                started[half],
-                (casts_a, casts_b)[half][number, 1, :, :size],
-                (seconds_a, seconds_b)[half].at[number],
-                size,
-            )
+            total = finish(started[half], (casts_a, casts_b)[half][number, 1, :, :size])
             out.append([total[:, t * WIN : (t + 1) * WIN] for t in range(size // WIN)])
-            sent.extend(started[half])
+            sent.append(started[half])
         return out
 
     pl.semaphore_wait(barrier, len(peers))
@@ -521,7 +515,7 @@
         remote(halo_src.at[1], halo_dst.at[1], edge_send.at[1], edge_recv.at[1], left)
     )
     copies[-1].start()
-    sent += [(0, copy) for copy in copies]
+    sent += copies
 
     def one_hot(slot):
         wide = lax.broadcasted_iota(jnp.int32, (TAPROWS, 36), 0)
@@ -637,19 +631,22 @@
         squares = sum(g * g for g in gradient)
         square = jnp.sum(jnp.sum(squares, axis=1, keepdims=True), axis=0, keepdims=True)
         square_src[number] = jnp.broadcast_to(square, (1, WIN))
-        spread_square = []
-        for by_inner, by_outer in everyone:
-            index = by_outer * inner + by_inner - 1
-            copy = remote(
-                square_src.at[number],
-                square_dst.at[number, index],
-                square_send.at[number, index],
-                square_recv.at[number, index],
-                lax.rem(my_outer + by_outer, outer) * inner + lax.rem(my_inner + by_inner, inner),
-            )
-            copy.start()
-            spread_square.append((index, copy))
-        sent += spread_square
+        spread_square = Batch(
+            [
+                remote(
+                    square_src.at[number],
+                    square_dst.at[number, by_outer * inner + by_inner - 1],
+                    square_send.at[number],
+                    square_recv.at[number],
+                    lax.rem(my_outer + by_outer, outer) * inner + lax.rem(my_inner + by_inner, inner),
+                )
+                for by_inner, by_outer in everyone
+            ],
+            square_dst.at[number],
+            square_send.at[number],
+            square_recv.at[number],
+        )
+        sent.append(spread_square)
 
         grads = pieces_of(gradient)
         if not last:
@@ -686,7 +683,7 @@
             right,
         )
         to_right.start()
-        sent.append((0, to_right))
+        sent.append(to_right)
         if not last:
             put(sums_left_src, (0,), base_own)
             put(sums_left_src, (1,), grad_own)
@@ -694,7 +691,7 @@
                 sums_left_src, sums_left_dst, edge_send.at[6], edge_recv.at[6], left
             )
             to_left.start()
-            sent.append((0, to_left))
+            sent.append(to_left)
 
         if not last:
             started = cast_middle(1, started)
@@ -717,24 +714,22 @@
             ]
             next_grad = [(g + c) * per_next for g, c in zip(grad_next, grad_far)]
             parts = (windows_of(own_base, next_base), windows_of(own_grad, next_grad))
-        for _, copy in spread_square:
-            copy.wait_recv()
+        spread_square.wait_recv()
         total = square_src[number] + jnp.sum(square_dst[number], axis=0)
         entries = 2 * count * 4 * HEIGHT * WIN
-        scale = guidance_ref[0, 0] * lax.rsqrt(total * (1.0 / entries) + STABILITY)
+        scale = guidance_ref[0] * lax.rsqrt(total * (1.0 / entries) + STABILITY)
         scale = (next_a / now_a) * scale
         tiles = [b - scale * g for b, g in zip(*parts)]
 
     for tile in range(HALF):
         out_ref[pl.ds(tile, 4, stride=8), :] = tiles[tile][:4]
         out_ref[pl.ds(tile + HALF, 4, stride=8), :] = tiles[tile][4:]
-    for _, copy in sent:
+    for copy in sent:
         copy.wait_send()
 
 
 def local(count, latent, noise, offsets, anchors, guidance, w_in, w_mid, w_out, t_embed, w_feat):
     inner, outer = group_sizes(count)
-    most = max(inner, outer)
     vmem = pl.BlockSpec(memory_space=pltpu.VMEM)
     block = HALF * WIN
     dma = pltpu.SemaphoreType.DMA
@@ -748,7 +743,7 @@
             pltpu.VMEM((STEPS * 32, WIN), F32),
             pltpu.SMEM((2,), jnp.int32),
             pltpu.SMEM((STEPS,), jnp.int32),
-            pltpu.SMEM((1, 1), F32),
+            pltpu.SMEM((1,), F32),
             pltpu.VMEM((36, HID), BF16),
             pltpu.VMEM((HID, HID), BF16),
             pltpu.VMEM((36, HID), BF16),
@@ -786,10 +781,10 @@
             pltpu.VMEM((STEPS, count - 1, 1, WIN), F32),
             dma((7,)),
             dma((7,)),
-            dma((STEPS, 2, 2, most - 1)),
-            dma((STEPS, 2, 2, most - 1)),
-            dma((STEPS, count - 1)),
-            dma((STEPS, count - 1)),
+            dma((STEPS, 2, 2)),
+            dma((STEPS, 2, 2)),
+            dma((STEPS,)),
+            dma((STEPS,)),
             dma((10,)),
         ],
         compiler_params=pltpu.CompilerParams(collective_id=0, has_side_effects=True),
@@ -799,7 +794,7 @@
         noise.reshape(STEPS * 32, WIN),
         offsets,
         anchors,
-        guidance.reshape(1, 1),
+        guidance,
         w_in.T,
         w_mid,
         w_out,

time: 50.3 us -> 46.7 us (0.928)
  Pallas kernels: 48.2 us -> 44.6 us
    pallas_call x1, Pallas kernels: 48.2 us -> 44.6 us  [local(): pl.pallas_call(functools.partial(kernel, count), out_shape=jax.ShapeDtype...]
where the time goes in v6:
time: 46.7 us; the launch traced here: 46.5 us
  Pallas kernels  44.6 us (96%)
  local copies, waits for them, and re-layouts  1.32 us (3%)
  between operations  0.66 us (1%)
    pallas_call x1, Pallas kernels, local(): pl.pallas_call(functools.partial(kernel, count), out_shape=jax.ShapeDtype...  44.6 us
    unnamed x1, local copies, waits for them, and re-layouts  1.32 us

profile of v6, /device:TPU:2, one launch (start us, length us, event | category | flops | bytes accessed | tf_op | source)
XLA Modules:
  0.0 46.5 jit_solution(12167422564953970179)
XLA Ops:
  0.7 44.6 %panorama.1 = f32[32,128]{1,0:T(8,128)} custom-call(f32[32,128]{1,0:T(8,128)} %bitcast.8, f32[64,128]{1,0:T(8,128)} %bitcast.6, s32[2]{0:T(128)} %offsets_hbm.1, s32[2]{0:T(128)} %anchors_hbm.1, f32[1]{0:T(128)S(6)} %copy.12.guidance_hbm, bf16[36,320]{1,0:T(8,128)(2,1)} %bitcast.7, bf16[320,320]{1,0:T(8,128)(2,1)} %w_mid_hbm.1, bf16[36,320]{1,0:T(8,128)(2,1)} %w_out_hbm.1, ...), custom_call_target="tpu_custom_call" | custom-call | tf_op jit(solution)/shard_map/panorama/pallas_call | solution.py:736
  45.2 1.3 %copy.13 = f32[4,8,128]{2,1,0:T(8,128)} copy(f32[4,8,128]{2,1,0:T(8,128)} %bitcast.5) | data formatting | bytes 32768

commit v7 on v6

--- a/solution.py
+++ b/solution.py
@@ -17,6 +17,7 @@
 HID = 320
 FEAT = 64
 TAPROWS = 80
+VMEM_LIMIT = 56520000
 ONES = 72
 BOTH = (512, 2)
 ALONE = (512, 1)
@@ -73,10 +74,10 @@
     return jnp.where(row_iota() < 4, low, high)
 
 
-def store_taps(ref, tiles, sign):
-    by_shift = {by: [sideways(tile, by) for tile in tiles] for by in (-1, 0, 1)}
+def tap_writer(ref, tile_of, sign):
     zero = jnp.zeros((ROWS, WIN), F32)
     one = jnp.ones((ROWS, WIN), F32)
+    shifted = {}
 
     def piece(k, h):
         if k >= len(TAP_SHIFTS):
@@ -85,31 +86,28 @@
         at = h + sign * down_by
         if at < 0 or at >= HEIGHT:
             return zero
-        return by_shift[sign * right_by][at]
-
-    for h in range(HEIGHT):
+        if at not in shifted:
+            shifted[at] = {by: sideways(tile_of(at), by) for by in (-1, 0, 1)}
+        return shifted[at][sign * right_by]
+
+    def write(h):
         for pair in range(TAPROWS // 16):
             both = jnp.concatenate([piece(2 * pair, h), piece(2 * pair + 1, h)], axis=0)
             ref[16 * pair : 16 * pair + 16, h * WIN : (h + 1) * WIN] = both.astype(BF16)
 
-
-def summed_taps(ref, sign, rounded):
-    tiles = []
-    for h in range(HEIGHT):
-        by_shift = {}
-        for k, (down_by, right_by) in enumerate(TAP_SHIFTS):
-            at = h + sign * down_by
-            if at < 0 or at >= HEIGHT:
-                continue
-            value = ref[8 * k : 8 * k + 8, at * WIN : (at + 1) * WIN]
-            if rounded:
-                value = value.astype(BF16).astype(F32)
-            shift = sign * right_by
-            by_shift[shift] = value if shift not in by_shift else by_shift[shift] + value
-        tiles.append(
-            by_shift[0] + sideways(by_shift[-1], -1) + sideways(by_shift[1], 1)
-        )
-    return tiles
+    return write
+
+
+def summed_taps(ref, sign, h):
+    by_shift = {}
+    for k, (down_by, right_by) in enumerate(TAP_SHIFTS):
+        at = h + sign * down_by
+        if at < 0 or at >= HEIGHT:
+            continue
+        value = ref[8 * k : 8 * k + 8, at * WIN : (at + 1) * WIN]
+        shift = sign * right_by
+        by_shift[shift] = value if shift not in by_shift else by_shift[shift] + value
+    return by_shift[0] + sideways(by_shift[-1], -1) + sideways(by_shift[1], 1)
 
 
 def silu_of_half(half):
@@ -170,7 +168,6 @@
     outward_ref,
     d1_ref,
     d2_ref,
-    percept_ref,
     active_ref,
     slope_ref,
     halo_src,
@@ -309,14 +306,25 @@
     put(casts_a, (0, 0), [own[0] * whole, own[1] * whole, halves[0], share])
     put(casts_b, (0, 0), [own[2] * whole, own[3] * whole, halves[1]])
 
-    def denoised(tiles, number, slots, keep):
-        store_taps(taps_ref, tiles, 1)
+    def ready(step, slot, chunk, slots, sign, use):
+        if slot == slots[-1]:
+            tall = chunk // WIN
+            start = max(0, step * tall - 1)
+            end = HEIGHT if (step + 1) * tall == HEIGHT else (step + 1) * tall - 1
+            for h in range(start, end):
+                use(h, summed_taps(outward_ref, sign, h))
+
+    def denoised(tile_of, number, slots, keep, use):
+        write_taps = tap_writer(taps_ref, tile_of, 1)
         chunk, apart = BOTH if keep else ALONE
         units = [(step, slot) for step in range(HEIGHT * WIN // chunk) for slot in slots]
         held, totals = {}, {}
 
         def stage_in(step, slot):
             at = slice(step * chunk, (step + 1) * chunk)
+            if slot == slots[0]:
+                for h in range(step * chunk // WIN, (step + 1) * chunk // WIN):
+                    write_taps(h)
             hidden = dot(win_ref[number, slot], taps_ref[:, at])
             half = hidden.astype(BF16)
             active, slope = silu_of_half(half)
@@ -339,17 +347,22 @@
             if slot == slots[-1]:
                 outward_ref[:, step * chunk : (step + 1) * chunk] = totals[step]
 
-        in_turn(units, (stage_in, stage_mid, stage_out), apart)
-        return summed_taps(outward_ref, 1, False)
-
-    def pulled_back(tiles):
-        store_taps(taps_ref, tiles, -1)
+        def stage_use(step, slot):
+            ready(step, slot, chunk, slots, 1, use)
+
+        in_turn(units, (stage_in, stage_mid, stage_out, stage_use), apart)
+
+    def pulled_back(tile_of, use):
+        write_taps = tap_writer(taps_ref, tile_of, -1)
         chunk, apart = BACK
         units = [(step, slot) for step in range(HEIGHT * WIN // chunk) for slot in range(2)]
         held, totals = {}, {}
 
         def stage_out(step, slot):
             at = slice(step * chunk, (step + 1) * chunk)
+            if slot == 0:
+                for h in range(step * chunk // WIN, (step + 1) * chunk // WIN):
+                    write_taps(h)
             joined = dot(woutt_ref[slot], taps_ref[:, at]).astype(BF16)
             held[step, slot] = (joined, joined * d2_ref[slot, :, at])
 
@@ -365,8 +378,10 @@
             if slot == 1:
                 outward_ref[:, step * chunk : (step + 1) * chunk] = totals[step]
 
-        in_turn(units, (stage_out, stage_mid, stage_in), apart)
-        return summed_taps(outward_ref, -1, False)
+        def stage_use(step, slot):
+            ready(step, slot, chunk, (0, 1), -1, use)
+
+        in_turn(units, (stage_out, stage_mid, stage_in, stage_use), apart)
 
     def features(tile, slot):
         total = None
@@ -561,11 +576,19 @@
     for number in range(STEPS):
         now_a, now_s, next_a, direction, spread = plan(number)
         last = number == STEPS - 1
-        predicted = denoised(tiles, number, (0, 1), True)
-        cleaned = [(x - now_s * p) * (1.0 / now_a) for x, p in zip(tiles, predicted)]
-        base = pieces_of(
-            [(next_a / now_a) * (x - now_s * p) + direction * p for x, p in zip(tiles, predicted)]
-        )
+        blend = [None] * HEIGHT
+
+        def own_use(h, predicted):
+            rest = tiles[h] - now_s * predicted
+            blend[h] = (next_a / now_a) * rest + direction * predicted
+            clean = rest * (1.0 / now_a)
+            for slot in range(2):
+                active, slope = silu_of_half(features(clean, slot))
+                active_ref[slot, h] = active
+                slope_ref[slot, h] = slope
+
+        denoised(lambda h: tiles[h], number, (0, 1), True, own_use)
+        base = pieces_of(blend)
         base_own, base_next = placed(base)
         if number == 0:
             for copy in copies[1:]:
@@ -574,12 +597,6 @@
             per_own = 1.0 / count_own
             per_next = 1.0 / (cover_next + cover_dst[0])
             noise_next = got(halo_dst, 1)
-
-        for slot in range(2):
-            for h in range(HEIGHT):
-                active, slope = silu_of_half(features(cleaned[h], slot))
-                active_ref[slot, h] = active
-                slope_ref[slot, h] = slope
 
         totals = cast_end(number, started)
         if number == 0:
@@ -605,29 +622,55 @@
                 ahead = shared[gap + 3 : gap + 4, :] - shared[3:4, :] + float(gap * STRIDE)
                 counted = counted + flag((places >= ahead) & (places < ahead + WIN))
             per_anchor = 1.0 / counted
+            width = count * WIN
+            origin = owners[1] * WIN + anchor_starts[1]
+
+            def apart(column):
+                return lax.rem(column - origin + width + width // 2, width) - width // 2
+
+            def framed(packed_tiles, by):
+                turn = lax.rem(by + width, WIN)
+                inside = (lanes >= by) & (lanes < by + WIN)
+                return [jnp.where(inside, pltpu.roll(t, turn, 1), 0.0) for t in packed_tiles]
+
+            gaps = [apart(me * WIN + start) for start in starts]
+            parts = [framed(piece, gap) for piece, gap in zip(base, gaps)]
+            parts.append(framed([spread * n * count_own for n in noise[0]], apart(me * WIN)))
+            base_part = [a + b + c for a, b, c in zip(*parts)]
         else:
             picked = [
                 (totals[t // 2][t % 2] - scale * totals[t // 2][2 + t % 2]) * per_anchor
                 for t in range(HALF)
             ]
         anchor_tiles = picked + [swapped(tile) for tile in picked]
-        anchor_predicted = denoised(anchor_tiles, number, (0,), False)
-        for h in range(HEIGHT):
-            clean = (anchor_tiles[h] - now_s * anchor_predicted[h]) * (1.0 / now_a)
-            percept_ref[h] = silu_of_half(features(clean, 0))[0]
-
-        clean_grad = []
-        for h in range(HEIGHT):
+        clean_grad = [None] * HEIGHT
+
+        def anchor_use(h, predicted):
+            clean = (anchor_tiles[h] - now_s * predicted) * (1.0 / now_a)
+            percept = silu_of_half(features(clean, 0))[0]
             grad = jnp.zeros((ROWS, WIN), F32)
             for slot in range(2):
-                pull = (active_ref[slot, h] - percept_ref[h]) * slope_ref[slot, h]
+                pull = (active_ref[slot, h] - percept) * slope_ref[slot, h]
                 for channel in range(4):
                     row = jnp.sum(feat_ref[channel] * pull, axis=0, keepdims=True)
                     grad = jnp.where(row_iota() == slot * 4 + channel, row, grad)
-            clean_grad.append(grad)
-        pulled = pulled_back([(-now_s / now_a / FEAT) * grad for grad in clean_grad])
-        gradient = [2.0 * p + g * (1.0 / now_a / FEAT) for p, g in zip(pulled, clean_grad)]
-
+            clean_grad[h] = grad
+
+        denoised(lambda h: anchor_tiles[h], number, (0,), False, anchor_use)
+        gradient = [None] * HEIGHT
+
+        def back_use(h, pulled):
+            gradient[h] = 2.0 * pulled + clean_grad[h] * (1.0 / now_a / FEAT)
+
+        pulled_back(lambda h: (-now_s / now_a / FEAT) * clean_grad[h], back_use)
+        grads = pieces_of(gradient)
+        if not last:
+            grad_part = [
+                a + b for a, b in zip(*[framed(piece, gap) for piece, gap in zip(grads, gaps)])
+            ]
+            put(casts_a, (1, 0), base_part[:2] + grad_part[:2])
+            put(casts_b, (1, 0), base_part[2:] + grad_part[2:])
+            started = cast_start(1)
         squares = sum(g * g for g in gradient)
         square = jnp.sum(jnp.sum(squares, axis=1, keepdims=True), axis=0, keepdims=True)
         square_src[number] = jnp.broadcast_to(square, (1, WIN))
@@ -647,30 +690,6 @@
             square_recv.at[number],
         )
         sent.append(spread_square)
-
-        grads = pieces_of(gradient)
-        if not last:
-            width = count * WIN
-            origin = owners[1] * WIN + anchor_starts[1]
-
-            def apart(column):
-                return lax.rem(column - origin + width + width // 2, width) - width // 2
-
-            def framed(packed_tiles, by):
-                turn = lax.rem(by + width, WIN)
-                inside = (lanes >= by) & (lanes < by + WIN)
-                return [jnp.where(inside, pltpu.roll(t, turn, 1), 0.0) for t in packed_tiles]
-
-            gaps = [apart(me * WIN + start) for start in starts]
-            parts = [framed(piece, gap) for piece, gap in zip(base, gaps)]
-            parts.append(framed([spread * n * count_own for n in noise[0]], apart(me * WIN)))
-            base_part = [a + b + c for a, b, c in zip(*parts)]
-            grad_part = [
-                a + b for a, b in zip(*[framed(piece, gap) for piece, gap in zip(grads, gaps)])
-            ]
-            put(casts_a, (1, 0), base_part[:2] + grad_part[:2])
-            put(casts_b, (1, 0), base_part[2:] + grad_part[2:])
-            started = cast_start(1)
 
         grad_own, grad_next = placed(grads)
         put(sums_right_src, (number, 0), base_next)
@@ -760,7 +779,6 @@
             pltpu.VMEM((TAPROWS, HEIGHT * WIN), F32),
             pltpu.VMEM((2, HID, HEIGHT * WIN), BF16),
             pltpu.VMEM((2, HID, HEIGHT * WIN), BF16),
-            pltpu.VMEM((HEIGHT, FEAT, WIN), F32),
             pltpu.VMEM((2, HEIGHT, FEAT, WIN), F32),
             pltpu.VMEM((2, HEIGHT, FEAT, WIN), F32),
             pltpu.VMEM((2, ROWS, block), F32),
@@ -787,7 +805,7 @@
             dma((STEPS,)),
             dma((10,)),
         ],
-        compiler_params=pltpu.CompilerParams(collective_id=0, has_side_effects=True),
+        compiler_params=pltpu.CompilerParams(collective_id=0, has_side_effects=True, vmem_limit_bytes=VMEM_LIMIT),
         name="panorama",
     )(
         latent.reshape(32, WIN),

time: 46.7 us -> 45.9 us (0.983)
  Pallas kernels: 44.6 us -> 43.7 us
    pallas_call x1, Pallas kernels: 44.6 us -> 43.7 us  [local(): pl.pallas_call(functools.partial(kernel, count), out_shape=jax.ShapeDtype...]
    unnamed x1 -> x9, local copies, waits for them, and re-layouts: 1.32 us -> 1.29 us
where the time goes in v7:
time: 45.9 us; the launch traced here: 45.7 us
  Pallas kernels  43.7 us (95%)
  local copies, waits for them, and re-layouts  1.29 us (3%)
  between operations  0.69 us (2%)
    pallas_call x1, Pallas kernels, local(): pl.pallas_call(functools.partial(kernel, count), out_shape=jax.ShapeDtype...  43.7 us
    unnamed x9, local copies, waits for them, and re-layouts  1.29 us

profile of v7, /device:TPU:2, one launch (start us, length us, event | category | flops | bytes accessed | tf_op | source)
XLA Modules:
  0.0 45.7 jit_solution(15493246927262000036)
XLA Ops:
  0.7 0.0 copy-start.3
  0.7 0.0 copy-start
  0.7 0.0 copy-start.1
  0.7 0.0 copy-start.2
  0.7 0.6 %copy-done.3 = s32[2]{0:T(128)S(1)} copy-done((s32[2]{0:T(128)S(1)}, s32[2]{0:T(128)}, u32[]{:S(2)}) %copy-start.3) | copy-done | bytes 32
  1.3 0.0 copy-done
  1.4 0.0 copy-done.1
  1.4 0.0 copy-done.2
  1.4 43.7 %panorama.1 = f32[32,128]{1,0:T(8,128)S(1)} custom-call(f32[32,128]{1,0:T(8,128)} %bitcast.9, f32[64,128]{1,0:T(8,128)} %bitcast.7, s32[2]{0:T(128)S(1)} %copy-done.2, s32[2]{0:T(128)S(1)} %copy-done.3, f32[1]{0:T(128)S(6)} %copy.12.guidance_hbm, bf16[36,320]{1,0:T(8,128)(2,1)} %bitcast.8, bf16[320,320]{1,0:T(8,128)(2,1)} %w_mid_hbm.1, ...), custom_call_target="tpu_custom_call" | custom-call | tf_op jit(solution)/shard_map/panorama/pallas_call | solution.py:755
  45.1 0.6 %copy.13 = f32[4,8,128]{2,1,0:T(8,128)} copy(f32[4,8,128]{2,1,0:T(8,128)S(1)} %bitcast.5) | data formatting | bytes 32768
Async XLA Ops:
  0.7 0.7 %copy-start.3 = (s32[2]{0:T(128)S(1)}, s32[2]{0:T(128)}, u32[]{:S(2)}) copy-start(s32[2]{0:T(128)} %anchors_hbm.1) | copy-start | bytes 28
  0.7 0.7 %copy-start = (f32[2,320]{1,0:T(2,128)S(1)}, f32[2,320]{1,0:T(2,128)}, u32[]{:S(2)}) copy-start(f32[2,320]{1,0:T(2,128)} %t_embed_hbm.1) | copy-start | bytes 7684
  0.7 0.7 %copy-start.1 = (f32[64,4]{0,1:T(4,128)S(1)}, f32[64,4]{0,1:T(4,128)}, u32[]{:S(2)}) copy-start(f32[64,4]{0,1:T(4,128)} %param.19) | copy-start | bytes 3076
  0.7 0.7 %copy-start.2 = (s32[2]{0:T(128)S(1)}, s32[2]{0:T(128)}, u32[]{:S(2)}) copy-start(s32[2]{0:T(128)} %offsets_hbm.1) | copy-start | bytes 28

commit v8 on v7

--- a/solution.py
+++ b/solution.py
@@ -11,6 +11,7 @@
 WIN = 128
 STRIDE = 64
 STEPS = 2
+CASTS = 3
 ROWS = 8
 HEIGHT = 8
 HALF = 4
@@ -209,7 +210,7 @@
         return lax.rem(my_outer + by, outer) * inner + my_inner
 
     barrier = pltpu.get_barrier_semaphore()
-    peers = [inner_peer(by) for by in range(1, inner)]
+    peers = [inner_peer(by) for by in sorted(range(1, inner), key=lambda by: abs(2 * by - inner))]
     peers += [outer_peer(by) for by in range(1, outer)]
     peers += [left, right]
     for peer in peers:
@@ -441,8 +442,15 @@
         key=lambda by: -min(by[0], inner - by[0]) - min(by[1] % 4, 4 - by[1] % 4) - by[1] // 4
     )
 
-    def far_first(size):
-        return sorted(range(1, size), key=lambda by: -min(by, size - by))
+    def far_first(along_inner):
+        size = inner if along_inner else outer
+
+        def hops(by):
+            if along_inner or size < 8:
+                return min(by, size - by)
+            return max(min(by % 4, 4 - by % 4) + 2 * (by // 4), (0, 3, 4, 3)[by % 4])
+
+        return sorted(range(1, size), key=lambda by: -hops(by))
 
     class Batch:
         def __init__(self, copies, landing, send, recv):
@@ -458,7 +466,7 @@
 
     def exchange(along_inner, source, target, send, recv):
         copies = []
-        for by in far_first(inner if along_inner else outer):
+        for by in far_first(along_inner):
             peer = inner_peer(by) if along_inner else outer_peer(by)
             copies.append(remote(source, target.at[by - 1], send, recv, peer))
         return Batch(copies, target, send, recv)
@@ -472,7 +480,7 @@
     sent = []
 
     def width_of(number, half):
-        return (HALF - 1 if number == 0 and half == 1 else HALF) * WIN
+        return (((HALF, HALF - 1), (2, 2), (2, 2))[number][half]) * WIN
 
     def cast_start(number):
         return [
@@ -598,7 +606,7 @@
             per_next = 1.0 / (cover_next + cover_dst[0])
             noise_next = got(halo_dst, 1)
 
-        totals = cast_end(number, started)
+        totals = cast_end(2 * number, started)
         if number == 0:
             shared = totals[0][3]
             anchor_starts = [
@@ -637,9 +645,13 @@
             parts = [framed(piece, gap) for piece, gap in zip(base, gaps)]
             parts.append(framed([spread * n * count_own for n in noise[0]], apart(me * WIN)))
             base_part = [a + b + c for a, b, c in zip(*parts)]
+            put(casts_a, (1, 0), base_part[:2])
+            put(casts_b, (1, 0), base_part[2:])
+            base_started = cast_start(1)
         else:
+            bases = cast_end(1, base_started)
             picked = [
-                (totals[t // 2][t % 2] - scale * totals[t // 2][2 + t % 2]) * per_anchor
+                (bases[t // 2][t % 2] - scale * totals[t // 2][t % 2]) * per_anchor
                 for t in range(HALF)
             ]
         anchor_tiles = picked + [swapped(tile) for tile in picked]
@@ -663,14 +675,6 @@
             gradient[h] = 2.0 * pulled + clean_grad[h] * (1.0 / now_a / FEAT)
 
         pulled_back(lambda h: (-now_s / now_a / FEAT) * clean_grad[h], back_use)
-        grads = pieces_of(gradient)
-        if not last:
-            grad_part = [
-                a + b for a, b in zip(*[framed(piece, gap) for piece, gap in zip(grads, gaps)])
-            ]
-            put(casts_a, (1, 0), base_part[:2] + grad_part[:2])
-            put(casts_b, (1, 0), base_part[2:] + grad_part[2:])
-            started = cast_start(1)
         squares = sum(g * g for g in gradient)
         square = jnp.sum(jnp.sum(squares, axis=1, keepdims=True), axis=0, keepdims=True)
         square_src[number] = jnp.broadcast_to(square, (1, WIN))
@@ -690,6 +694,15 @@
             square_recv.at[number],
         )
         sent.append(spread_square)
+
+        grads = pieces_of(gradient)
+        if not last:
+            grad_part = [
+                a + b for a, b in zip(*[framed(piece, gap) for piece, gap in zip(grads, gaps)])
+            ]
+            put(casts_a, (2, 0), grad_part[:2])
+            put(casts_b, (2, 0), grad_part[2:])
+            started = cast_start(2)
 
         grad_own, grad_next = placed(grads)
         put(sums_right_src, (number, 0), base_next)
@@ -713,7 +726,8 @@
             sent.append(to_left)
 
         if not last:
-            started = cast_middle(1, started)
+            base_started = cast_middle(1, base_started)
+            started = cast_middle(2, started)
         to_right.wait_recv()
         base_in = got(sums_right_dst, number, 0)
         grad_in = got(sums_right_dst, number, 1)
@@ -789,18 +803,18 @@
             pltpu.VMEM((2, ROWS, block), F32),
             pltpu.VMEM((STEPS, 2, ROWS, block), F32),
             pltpu.VMEM((STEPS, 2, ROWS, block), F32),
-            pltpu.VMEM((STEPS, 2, ROWS, block), F32),
-            pltpu.VMEM((STEPS, 2, ROWS, block), F32),
-            pltpu.VMEM((STEPS, inner - 1, ROWS, block), F32),
-            pltpu.VMEM((STEPS, outer - 1, ROWS, block), F32),
-            pltpu.VMEM((STEPS, outer - 1, ROWS, block), F32),
-            pltpu.VMEM((STEPS, inner - 1, ROWS, block), F32),
+            pltpu.VMEM((CASTS, 2, ROWS, block), F32),
+            pltpu.VMEM((CASTS, 2, ROWS, block), F32),
+            pltpu.VMEM((CASTS, inner - 1, ROWS, block), F32),
+            pltpu.VMEM((CASTS, outer - 1, ROWS, block), F32),
+            pltpu.VMEM((CASTS, outer - 1, ROWS, block), F32),
+            pltpu.VMEM((CASTS, inner - 1, ROWS, block), F32),
             pltpu.VMEM((STEPS, 1, WIN), F32),
             pltpu.VMEM((STEPS, count - 1, 1, WIN), F32),
             dma((7,)),
             dma((7,)),
-            dma((STEPS, 2, 2)),
-            dma((STEPS, 2, 2)),
+            dma((CASTS, 2, 2)),
+            dma((CASTS, 2, 2)),
             dma((STEPS,)),
             dma((STEPS,)),
             dma((10,)),

time: 45.9 us -> 45.9 us (level)
  no operation moved by 1% of the time
where the time goes in v8:
time: 45.9 us; the launch traced here: 45.7 us
  Pallas kernels  43.7 us (95%)
  local copies, waits for them, and re-layouts  1.29 us (3%)
  between operations  0.69 us (2%)
    pallas_call x1, Pallas kernels, local(): pl.pallas_call(functools.partial(kernel, count), out_shape=jax.ShapeDtype...  43.7 us
    unnamed x9, local copies, waits for them, and re-layouts  1.29 us

profile of v8, /device:TPU:2, one launch (start us, length us, event | category | flops | bytes accessed | tf_op | source)
XLA Modules:
  0.0 45.7 jit_solution(15230083123665165942)
XLA Ops:
  0.7 0.0 copy-start.3
  0.7 0.0 copy-start
  0.7 0.0 copy-start.1
  0.7 0.0 copy-start.2
  0.7 0.6 %copy-done.3 = s32[2]{0:T(128)S(1)} copy-done((s32[2]{0:T(128)S(1)}, s32[2]{0:T(128)}, u32[]{:S(2)}) %copy-start.3) | copy-done | bytes 32
  1.3 0.0 copy-done
  1.4 0.0 copy-done.1
  1.4 0.0 copy-done.2
  1.4 43.7 %panorama.1 = f32[32,128]{1,0:T(8,128)S(1)} custom-call(f32[32,128]{1,0:T(8,128)} %bitcast.9, f32[64,128]{1,0:T(8,128)} %bitcast.7, s32[2]{0:T(128)S(1)} %copy-done.2, s32[2]{0:T(128)S(1)} %copy-done.3, f32[1]{0:T(128)S(6)} %copy.12.guidance_hbm, bf16[36,320]{1,0:T(8,128)(2,1)} %bitcast.8, bf16[320,320]{1,0:T(8,128)(2,1)} %w_mid_hbm.1, ...), custom_call_target="tpu_custom_call" | custom-call | tf_op jit(solution)/shard_map/panorama/pallas_call | solution.py:769
  45.1 0.6 %copy.13 = f32[4,8,128]{2,1,0:T(8,128)} copy(f32[4,8,128]{2,1,0:T(8,128)S(1)} %bitcast.5) | data formatting | bytes 32768
Async XLA Ops:
  0.7 0.7 %copy-start.3 = (s32[2]{0:T(128)S(1)}, s32[2]{0:T(128)}, u32[]{:S(2)}) copy-start(s32[2]{0:T(128)} %anchors_hbm.1) | copy-start | bytes 28
  0.7 0.7 %copy-start = (f32[2,320]{1,0:T(2,128)S(1)}, f32[2,320]{1,0:T(2,128)}, u32[]{:S(2)}) copy-start(f32[2,320]{1,0:T(2,128)} %t_embed_hbm.1) | copy-start | bytes 7684
  0.7 0.7 %copy-start.1 = (f32[64,4]{0,1:T(4,128)S(1)}, f32[64,4]{0,1:T(4,128)}, u32[]{:S(2)}) copy-start(f32[64,4]{0,1:T(4,128)} %param.19) | copy-start | bytes 3076
  0.7 0.7 %copy-start.2 = (s32[2]{0:T(128)S(1)}, s32[2]{0:T(128)}, u32[]{:S(2)}) copy-start(s32[2]{0:T(128)} %offsets_hbm.1) | copy-start | bytes 28

commit v9 on v8

--- a/solution.py
+++ b/solution.py
@@ -675,6 +675,14 @@
             gradient[h] = 2.0 * pulled + clean_grad[h] * (1.0 / now_a / FEAT)
 
         pulled_back(lambda h: (-now_s / now_a / FEAT) * clean_grad[h], back_use)
+        grads = pieces_of(gradient)
+        if not last:
+            grad_part = [
+                a + b for a, b in zip(*[framed(piece, gap) for piece, gap in zip(grads, gaps)])
+            ]
+            put(casts_a, (2, 0), grad_part[:2])
+            put(casts_b, (2, 0), grad_part[2:])
+            started = cast_start(2)
         squares = sum(g * g for g in gradient)
         square = jnp.sum(jnp.sum(squares, axis=1, keepdims=True), axis=0, keepdims=True)
         square_src[number] = jnp.broadcast_to(square, (1, WIN))
@@ -694,15 +702,6 @@
             square_recv.at[number],
         )
         sent.append(spread_square)
-
-        grads = pieces_of(gradient)
-        if not last:
-            grad_part = [
-                a + b for a, b in zip(*[framed(piece, gap) for piece, gap in zip(grads, gaps)])
-            ]
-            put(casts_a, (2, 0), grad_part[:2])
-            put(casts_b, (2, 0), grad_part[2:])
-            started = cast_start(2)
 
         grad_own, grad_next = placed(grads)
         put(sums_right_src, (number, 0), base_next)
@@ -748,7 +747,10 @@
             next_grad = [(g + c) * per_next for g, c in zip(grad_next, grad_far)]
             parts = (windows_of(own_base, next_base), windows_of(own_grad, next_grad))
         spread_square.wait_recv()
-        total = square_src[number] + jnp.sum(square_dst[number], axis=0)
+        rows = [square_src[number]] + [square_dst[number, index] for index in range(count - 1)]
+        while len(rows) > 1:
+            rows = [sum(rows[at : at + 2]) for at in range(0, len(rows), 2)]
+        total = rows[0]
         entries = 2 * count * 4 * HEIGHT * WIN
         scale = guidance_ref[0] * lax.rsqrt(total * (1.0 / entries) + STABILITY)
         scale = (next_a / now_a) * scale

time: 45.9 us -> 45.4 us (0.989)
  Pallas kernels: 43.7 us -> 43.2 us
    pallas_call x1, Pallas kernels: 43.7 us -> 43.2 us  [local(): pl.pallas_call(functools.partial(kernel, count), out_shape=jax.ShapeDtype...]
where the time goes in v9:
time: 45.4 us; the launch traced here: 45.2 us
  Pallas kernels  43.2 us (95%)
  local copies, waits for them, and re-layouts  1.29 us (3%)
  between operations  0.69 us (2%)
    pallas_call x1, Pallas kernels, local(): pl.pallas_call(functools.partial(kernel, count), out_shape=jax.ShapeDtype...  43.2 us
    unnamed x9, local copies, waits for them, and re-layouts  1.29 us

profile of v9, /device:TPU:2, one launch (start us, length us, event | category | flops | bytes accessed | tf_op | source)
XLA Modules:
  0.0 45.2 jit_solution(7692773422917666393)
XLA Ops:
  0.7 0.0 copy-start.3
  0.7 0.0 copy-start
  0.7 0.0 copy-start.1
  0.7 0.0 copy-start.2
  0.7 0.6 %copy-done.3 = s32[2]{0:T(128)S(1)} copy-done((s32[2]{0:T(128)S(1)}, s32[2]{0:T(128)}, u32[]{:S(2)}) %copy-start.3) | copy-done | bytes 32
  1.3 0.0 copy-done
  1.4 0.0 copy-done.1
  1.4 0.0 copy-done.2
  1.4 43.2 %panorama.1 = f32[32,128]{1,0:T(8,128)S(1)} custom-call(f32[32,128]{1,0:T(8,128)} %bitcast.9, f32[64,128]{1,0:T(8,128)} %bitcast.7, s32[2]{0:T(128)S(1)} %copy-done.2, s32[2]{0:T(128)S(1)} %copy-done.3, f32[1]{0:T(128)S(6)} %copy.12.guidance_hbm, bf16[36,320]{1,0:T(8,128)(2,1)} %bitcast.8, bf16[320,320]{1,0:T(8,128)(2,1)} %w_mid_hbm.1, ...), custom_call_target="tpu_custom_call" | custom-call | tf_op jit(solution)/shard_map/panorama/pallas_call | solution.py:771
  44.6 0.6 %copy.13 = f32[4,8,128]{2,1,0:T(8,128)} copy(f32[4,8,128]{2,1,0:T(8,128)S(1)} %bitcast.5) | data formatting | bytes 32768
Async XLA Ops:
  0.7 0.7 %copy-start.3 = (s32[2]{0:T(128)S(1)}, s32[2]{0:T(128)}, u32[]{:S(2)}) copy-start(s32[2]{0:T(128)} %anchors_hbm.1) | copy-start | bytes 28
  0.7 0.7 %copy-start = (f32[2,320]{1,0:T(2,128)S(1)}, f32[2,320]{1,0:T(2,128)}, u32[]{:S(2)}) copy-start(f32[2,320]{1,0:T(2,128)} %t_embed_hbm.1) | copy-start | bytes 7684
  0.7 0.7 %copy-start.1 = (f32[64,4]{0,1:T(4,128)S(1)}, f32[64,4]{0,1:T(4,128)}, u32[]{:S(2)}) copy-start(f32[64,4]{0,1:T(4,128)} %param.19) | copy-start | bytes 3076
  0.7 0.7 %copy-start.2 = (s32[2]{0:T(128)S(1)}, s32[2]{0:T(128)}, u32[]{:S(2)}) copy-start(s32[2]{0:T(128)} %offsets_hbm.1) | copy-start | bytes 28

commit v10 on v9

--- a/solution.py
+++ b/solution.py
@@ -217,9 +217,9 @@
         pl.semaphore_signal(barrier, inc=1, device_id=(peer, part), device_id_type=MESH)
 
     pairs = [
+        (latent_hbm, latent_ref),
         (offsets_hbm, offsets_ref),
         (anchors_hbm, anchors_ref),
-        (latent_hbm, latent_ref),
         (noise_hbm, noise_ref),
         (w_in_hbm, w_in_ref),
         (w_mid_hbm, w_mid_ref),

time: 45.4 us -> 45.4 us (level)
  no operation moved by 1% of the time
where the time goes in v10:
time: 45.4 us; the launch traced here: 45.2 us
  Pallas kernels  43.2 us (95%)
  local copies, waits for them, and re-layouts  1.29 us (3%)
  between operations  0.69 us (2%)
    pallas_call x1, Pallas kernels, local(): pl.pallas_call(functools.partial(kernel, count), out_shape=jax.ShapeDtype...  43.2 us
    unnamed x9, local copies, waits for them, and re-layouts  1.29 us

profile of v10, /device:TPU:2, one launch (start us, length us, event | category | flops | bytes accessed | tf_op | source)
XLA Modules:
  0.0 45.2 jit_solution(5473034203953126064)
XLA Ops:
  0.7 0.0 copy-start.3
  0.7 0.0 copy-start
  0.7 0.0 copy-start.1
  0.7 0.0 copy-start.2
  0.7 0.6 %copy-done.3 = s32[2]{0:T(128)S(1)} copy-done((s32[2]{0:T(128)S(1)}, s32[2]{0:T(128)}, u32[]{:S(2)}) %copy-start.3) | copy-done | bytes 32
  1.3 0.0 copy-done
  1.4 0.0 copy-done.1
  1.4 0.0 copy-done.2
  1.4 43.2 %panorama.1 = f32[32,128]{1,0:T(8,128)S(1)} custom-call(f32[32,128]{1,0:T(8,128)} %bitcast.9, f32[64,128]{1,0:T(8,128)} %bitcast.7, s32[2]{0:T(128)S(1)} %copy-done.2, s32[2]{0:T(128)S(1)} %copy-done.3, f32[1]{0:T(128)S(6)} %copy.12.guidance_hbm, bf16[36,320]{1,0:T(8,128)(2,1)} %bitcast.8, bf16[320,320]{1,0:T(8,128)(2,1)} %w_mid_hbm.1, ...), custom_call_target="tpu_custom_call" | custom-call | tf_op jit(solution)/shard_map/panorama/pallas_call | solution.py:771
  44.6 0.6 %copy.13 = f32[4,8,128]{2,1,0:T(8,128)} copy(f32[4,8,128]{2,1,0:T(8,128)S(1)} %bitcast.5) | data formatting | bytes 32768
Async XLA Ops:
  0.7 0.7 %copy-start.3 = (s32[2]{0:T(128)S(1)}, s32[2]{0:T(128)}, u32[]{:S(2)}) copy-start(s32[2]{0:T(128)} %anchors_hbm.1) | copy-start | bytes 28
  0.7 0.7 %copy-start = (f32[2,320]{1,0:T(2,128)S(1)}, f32[2,320]{1,0:T(2,128)}, u32[]{:S(2)}) copy-start(f32[2,320]{1,0:T(2,128)} %t_embed_hbm.1) | copy-start | bytes 7684
  0.7 0.7 %copy-start.1 = (f32[64,4]{0,1:T(4,128)S(1)}, f32[64,4]{0,1:T(4,128)}, u32[]{:S(2)}) copy-start(f32[64,4]{0,1:T(4,128)} %param.19) | copy-start | bytes 3076
  0.7 0.7 %copy-start.2 = (s32[2]{0:T(128)S(1)}, s32[2]{0:T(128)}, u32[]{:S(2)}) copy-start(s32[2]{0:T(128)} %offsets_hbm.1) | copy-start | bytes 28
